TPU v7x, 128 devices: a whole 4x4x4 slice. The times are simulated.
128 devices in a mesh: section: 8 (over x, core), expert: 4 (over y), dp: 4 (over z).
Axes of the slice: x: 4, y: 4, z: 4, core: 2. Of those that a mesh axis runs over, the one named last changes fastest.
Arguments:
- x_in: bfloat16 [8, 256, 2048], P(None, ('expert', 'dp'), 'section'), may hold values from -6 to 6
- cotangent: bfloat16 [8, 256, 2048], P(None, ('expert', 'dp'), 'section'), may hold values from -6 to 6
- route_ids: int32 [8, 8, 256, 2], P('section', None, ('expert', 'dp')), may hold values from 0 to 15, all different within a row; in each aligned block of 16 rows (0 to 15, 16 to 31, ..., all dimensions but the last counted through in order) at most 2 rows name the same one
- norm_gain: float32 [8, 2048], P('section'), may hold values from 0.5 to 1.5
- router: bfloat16 [8, 2048, 16], P('section'), may hold values from -0.125 to 0.125
- w_gate_up: bfloat16 [8, 16, 2048, 1024], P('section', ('expert', 'dp')), may hold values from -0.125 to 0.125
- w_down: bfloat16 [8, 16, 512, 2048], P('section', ('expert', 'dp')), may hold values from -0.25 to 0.25
Outputs:
- grad_in: bfloat16 [8, 256, 2048], P(None, ('expert', 'dp'), 'section')
- grad_gate_up: float32 [8, 16, 2048, 1024], P('section', ('expert', 'dp'))
- grad_down: float32 [8, 16, 512, 2048], P('section', ('expert', 'dp'))
- grad_router: float32 [8, 2048, 16], P('section')
- grad_gain: float32 [8, 2048], P('section')
Inputs may be any that keep to these rules, and one draw needn't show every extreme that they name: `route_ids`: each row names two different experts; the 16 rows of one device in one layer and micro-batch name any expert at most 2 times, a bound that some block reaches in some of them.
All inputs are finite; a program needn't handle non-finite values.
Results may differ from a plain program's by a relative error of at most 0.035.
Values may be sent and summed in bfloat16 or wider, within the bound.
A program may use at most 64 MiB of HBM per device.

v0:
```python
import jax
import jax.numpy as jnp
from jax import lax
from jax.sharding import PartitionSpec as P

EPS = 1e-05


def sent_together(arrays, axis, dim, along):
    widths = [a.shape[along] for a in arrays]
    both = jnp.concatenate(arrays, axis=along)
    whole = lax.all_gather(both, axis, axis=dim, tiled=True)
    return tuple(jnp.split(whole, [sum(widths[:k]) for k in range(1, len(widths))], axis=along))


def shifted(value, axis, steps):
    count = lax.axis_size(axis)
    leading, last = (max(0, -steps), min(count, count - steps))
    return lax.ppermute(value, axis, [(source, source + steps) for source in range(leading, last)])


def copy_for_each(shard, axis):
    copies = jnp.broadcast_to(shard, (lax.axis_size(axis), *shard.shape))
    return lax.all_to_all(copies, axis, split_axis=0, concat_axis=0, tiled=True)


def of_everyone(shard, axis):
    return copy_for_each(shard, axis).astype(jnp.float32).sum(axis=0)


def in_blocks(shard, dim, length):
    before, after = (shard.shape[:dim], shard.shape[dim + 1 :])
    return jnp.moveaxis(shard.reshape(*before, length, -1, *after), dim, 0)


def sent_and_summed(shard, axis, dim):
    length = lax.axis_size(axis)
    pieces = lax.all_to_all(in_blocks(shard, dim, length), axis, 0, 0, tiled=True)
    return jnp.sum(pieces.astype(jnp.float32), axis=0)


def keep_row(stash, position, value, active):
    old_row = lax.dynamic_index_in_dim(stash, position, 0, keepdims=False)
    return lax.dynamic_update_index_in_dim(stash, jnp.where(active, value, old_row), position, 0)


def slot_tables(route_rows, n_expert, capacity):
    experts = jnp.arange(n_expert, dtype=jnp.int32)
    expert_hits = (route_rows[:, :, None] == experts).astype(jnp.int32)
    per_expert = jnp.sum(expert_hits, axis=1)
    before = jnp.cumsum(per_expert, axis=0) - per_expert
    slot_ids = jnp.sum(expert_hits * before[:, None, :], axis=2)
    dest_cell = jnp.transpose(route_rows * capacity + slot_ids)
    cell_ids = jnp.arange(n_expert * capacity, dtype=jnp.int32)
    slot_place = (dest_cell[:, :, None] == cell_ids).astype(jnp.bfloat16)
    return (expert_hits.astype(jnp.float32), slot_place)


def norm_rows(layer_in, gain_vec):
    h_wide = layer_in.astype(jnp.float32)
    inv_rms = lax.rsqrt(jnp.mean(h_wide * h_wide, axis=-1, keepdims=True) + EPS)
    normed = (h_wide * inv_rms * gain_vec).astype(jnp.bfloat16)
    return (h_wide, inv_rms, normed)


def pair_gates(normed, router_mat, expert_hits):
    logits = jnp.dot(normed, router_mat, preferred_element_type=jnp.float32)
    chosen = jnp.sum(expert_hits * logits[:, None, :], axis=2)
    return (
        jax.nn.sigmoid(chosen[:, 0] - chosen[:, 1]),
        jax.nn.sigmoid(chosen[:, 1] - chosen[:, 0]),
    )


def expert_inner(exp_rows, w_gu):
    gate_up = jnp.einsum("sekd,edf->sekf", exp_rows, w_gu, preferred_element_type=jnp.float32)
    half_cols = w_gu.shape[2] // 2
    gate_part = gate_up[..., :half_cols]
    up_part = gate_up[..., half_cols:]
    sigmoid_gate = jax.nn.sigmoid(gate_part)
    hidden = (gate_part * sigmoid_gate * up_part).astype(jnp.bfloat16)
    return (gate_part, up_part, sigmoid_gate, hidden)


def expert_grads(gate_part, up_part, sigmoid_gate, dy_rows, w_gu, w_dn):
    d_hidden = jnp.einsum("sekd,efd->sekf", dy_rows, w_dn, preferred_element_type=jnp.float32)
    silu_gate = gate_part * sigmoid_gate
    silu_slope = sigmoid_gate * (1.0 + gate_part * (1.0 - sigmoid_gate))
    gate_up_grad = jnp.concatenate(
        [d_hidden * up_part * silu_slope, d_hidden * silu_gate], axis=-1
    ).astype(jnp.bfloat16)
    rows_grad = jnp.einsum(
        "sekf,edf->sekd", gate_up_grad, w_gu, preferred_element_type=jnp.float32
    ).astype(jnp.bfloat16)
    return (gate_up_grad, rows_grad)


def local(x_in, cotangent, route_ids, norm_gain, router, w_gate_up, w_down):
    micro_count, tok_rows, _ = x_in.shape
    n_segment = lax.axis_size("section")
    n_rank = lax.axis_size("expert") * lax.axis_size("dp")
    per_rank = w_down.shape[1]
    hidden_width = w_down.shape[2]
    model_width = w_down.shape[3]
    n_expert = per_rank * n_rank
    capacity = tok_rows * 2 * 9 // (8 * n_expert)
    cells = n_expert * capacity
    segment_idx = lax.axis_index("section")
    rows_shape = (n_rank, per_rank, capacity, model_width)
    x_all, top_all = sent_together((x_in, cotangent), "section", 2, 0)
    route_all = route_ids[0]
    gain_vec = norm_gain[0]
    router_mat = router[0]
    router_wide = router_mat.astype(jnp.float32)
    w_gu = w_gate_up[0]
    w_dn = w_down[0]
    ticks = micro_count + n_segment - 1

    def expert_forward(piece_rows):
        _, _, _, hidden = expert_inner(piece_rows, w_gu)
        out_rows = jnp.einsum(
            "sekf,efd->sekd", hidden, w_dn, preferred_element_type=jnp.float32
        ).astype(jnp.bfloat16)
        return (
            lax.all_to_all(out_rows, ("expert", "dp"), split_axis=0, concat_axis=0, tiled=True),
            piece_rows,
        )

    def forward_tick(tick_no, state_in):
        received, stash_h, stash_y, stash_x = state_in
        tick_slot = tick_no - segment_idx
        active = (tick_slot >= 0) & (tick_slot < micro_count)
        micro_idx = jnp.clip(tick_slot, 0, micro_count - 1)
        fresh_in = lax.dynamic_index_in_dim(x_all, micro_idx, 0, keepdims=False)
        layer_in = jnp.where(segment_idx == 0, fresh_in, received)
        h_wide, inv_rms, normed = norm_rows(layer_in, gain_vec)
        route_rows = lax.dynamic_index_in_dim(route_all, micro_idx, 0, keepdims=False)
        expert_hits, slot_place = slot_tables(route_rows, n_expert, capacity)
        send_rows = jnp.einsum("ktc,td->cd", slot_place, normed, preferred_element_type=jnp.float32)
        send_rows = send_rows.astype(jnp.bfloat16).reshape(rows_shape)
        returned, landed = expert_forward(
            lax.all_to_all(send_rows, ("expert", "dp"), split_axis=0, concat_axis=0, tiled=True)
        )
        back_flat = returned.reshape(cells, model_width)
        picked = jnp.einsum(
            "ktc,cd->ktd", slot_place, back_flat, preferred_element_type=jnp.float32
        )
        first_gate, second_gate = pair_gates(normed, router_mat, expert_hits)
        layer_out = (
            h_wide + first_gate[:, None] * picked[0] + second_gate[:, None] * picked[1]
        ).astype(jnp.bfloat16)
        passed = shifted(layer_out, "section", 1)
        stash_h = keep_row(stash_h, micro_idx, layer_in, active)
        stash_y = keep_row(stash_y, micro_idx, back_flat, active)
        stash_x = keep_row(stash_x, micro_idx, landed, active)
        return (passed, stash_h, stash_y, stash_x)

    start_fwd = (
        jnp.zeros((tok_rows, model_width), jnp.bfloat16),
        jnp.zeros((micro_count, tok_rows, model_width), jnp.bfloat16),
        jnp.zeros((micro_count, cells, model_width), jnp.bfloat16),
        jnp.zeros((micro_count,) + rows_shape, jnp.bfloat16),
    )
    _, stash_h, stash_y, stash_x = lax.fori_loop(0, ticks, forward_tick, start_fwd)

    def backward_tick(tick_no, state_in):
        received, keep_rows, keep_dy, keep_hidden, keep_dab, stash_grad, acc_router, acc_gain = (
            state_in
        )
        tick_slot = tick_no - (n_segment - 1 - segment_idx)
        active = (tick_slot >= 0) & (tick_slot < micro_count)
        micro_idx = jnp.clip(tick_slot, 0, micro_count - 1)
        fresh_top = lax.dynamic_index_in_dim(top_all, micro_idx, 0, keepdims=False)
        grad_top = jnp.where(segment_idx == n_segment - 1, fresh_top, received)
        grad_wide = grad_top.astype(jnp.float32)
        layer_in = lax.dynamic_index_in_dim(stash_h, micro_idx, 0, keepdims=False)
        h_wide, inv_rms, normed = norm_rows(layer_in, gain_vec)
        route_rows = lax.dynamic_index_in_dim(route_all, micro_idx, 0, keepdims=False)
        expert_hits, slot_place = slot_tables(route_rows, n_expert, capacity)
        first_gate, second_gate = pair_gates(normed, router_mat, expert_hits)
        gates = jnp.stack([first_gate, second_gate])
        scaled = (gates[:, :, None] * grad_wide[None]).astype(jnp.bfloat16)
        dy_send = jnp.einsum("ktc,ktd->cd", slot_place, scaled, preferred_element_type=jnp.float32)
        dy_send = dy_send.astype(jnp.bfloat16).reshape(rows_shape)
        exp_rows = lax.dynamic_index_in_dim(stash_x, micro_idx, 0, keepdims=False)
        dy_rows = lax.all_to_all(dy_send, ("expert", "dp"), split_axis=0, concat_axis=0, tiled=True)
        gate_part, up_part, sigmoid_gate, hidden = expert_inner(exp_rows, w_gu)
        gate_up_grad, rows_grad = expert_grads(
            gate_part, up_part, sigmoid_gate, dy_rows, w_gu, w_dn
        )
        back_grad = lax.all_to_all(
            rows_grad, ("expert", "dp"), split_axis=0, concat_axis=0, tiled=True
        )
        back_y = lax.dynamic_index_in_dim(stash_y, micro_idx, 0, keepdims=False)
        keep_dy = keep_row(keep_dy, micro_idx, dy_rows, active)
        keep_hidden = keep_row(keep_hidden, micro_idx, hidden, active)
        keep_dab = keep_row(keep_dab, micro_idx, gate_up_grad, active)
        normed_grad = jnp.einsum(
            "ktc,cd->td",
            slot_place,
            back_grad.reshape(cells, model_width),
            preferred_element_type=jnp.float32,
        )
        picked = jnp.einsum("ktc,cd->ktd", slot_place, back_y, preferred_element_type=jnp.float32)
        gate_grad = jnp.sum(grad_wide[None] * picked, axis=-1)
        logit_grad = first_gate * second_gate * (gate_grad[0] - gate_grad[1])
        logit_cols = logit_grad[:, None] * (expert_hits[:, 0, :] - expert_hits[:, 1, :])
        normed_grad = normed_grad + jnp.dot(logit_cols, router_wide.T)
        router_term = jnp.dot(normed.astype(jnp.float32).T, logit_cols)
        acc_router = acc_router + jnp.where(active, router_term, 0.0)
        acc_gain = acc_gain + jnp.where(
            active, jnp.sum(normed_grad * h_wide * inv_rms, axis=0), 0.0
        )
        scaled_grad = normed_grad * gain_vec
        projection = jnp.mean(scaled_grad * h_wide, axis=-1, keepdims=True)
        input_grad = (
            grad_wide + inv_rms * scaled_grad - h_wide * inv_rms * inv_rms * inv_rms * projection
        )
        grad_sent = input_grad.astype(jnp.bfloat16)
        stash_grad = keep_row(stash_grad, micro_idx, grad_sent, active)
        passed = shifted(grad_sent, "section", -1)
        return (passed, keep_rows, keep_dy, keep_hidden, keep_dab, stash_grad, acc_router, acc_gain)

    start_bwd = (
        jnp.zeros((tok_rows, model_width), jnp.bfloat16),
        stash_x,
        jnp.zeros((micro_count,) + rows_shape, jnp.bfloat16),
        jnp.zeros((micro_count, n_rank, per_rank, capacity, hidden_width), jnp.bfloat16),
        jnp.zeros((micro_count, n_rank, per_rank, capacity, 2 * hidden_width), jnp.bfloat16),
        jnp.zeros((micro_count, tok_rows, model_width), jnp.bfloat16),
        jnp.zeros((model_width, n_expert), jnp.float32),
        jnp.zeros((model_width,), jnp.float32),
    )
    final = lax.fori_loop(0, ticks, backward_tick, start_bwd)
    _, keep_rows, keep_dy, keep_hidden, keep_dab, stash_grad, acc_router, acc_gain = final
    grad_gu = jnp.einsum(
        "msekd,msekf->edf", keep_rows, keep_dab, preferred_element_type=jnp.float32
    )
    grad_dn = jnp.einsum(
        "msekf,msekd->efd", keep_hidden, keep_dy, preferred_element_type=jnp.float32
    )
    sum_router, sum_gain = (
        of_everyone(acc_router.astype(jnp.bfloat16), ("expert", "dp")).astype(jnp.float32),
        of_everyone(acc_gain.astype(jnp.bfloat16), ("expert", "dp")).astype(jnp.float32),
    )
    first_term = jnp.where(segment_idx == 0, stash_grad.astype(jnp.float32), 0.0)
    grad_in = sent_and_summed(first_term.astype(jnp.bfloat16), "section", 2).astype(jnp.bfloat16)
    return (grad_in, grad_gu[None], grad_dn[None], sum_router[None], sum_gain[None])


def solution(mesh):
    in_specs = (
        P(None, ("expert", "dp"), "section"),
        P(None, ("expert", "dp"), "section"),
        P("section", None, ("expert", "dp"), None),
        P("section", None),
        P("section", None, None),
        P("section", ("expert", "dp"), None, None),
        P("section", ("expert", "dp"), None, None),
    )
    out_specs = (
        P(None, ("expert", "dp"), "section"),
        P("section", ("expert", "dp"), None, None),
        P("section", ("expert", "dp"), None, None),
        P("section", None, None),
        P("section", None),
    )
    return jax.shard_map(local, mesh=mesh, in_specs=in_specs, out_specs=out_specs, check_vma=False)
```

profile of v0, /device:TPU:0, one launch (start us, length us, event | category | flops | bytes accessed | tf_op | source)
XLA Modules:
  0.0 1300.0 jit_solution(4501914240552446879)
XLA Ops:
  9.0 27.0 %all-gather.2.cloned.1.call-done = bf16[16,16,2048]{2,1,0:T(8,128)(2,1)} async-done(((bf16[16,16,256]{2,1,0:T(8,128)(2,1)}), bf16[16,16,2048]{2,1,0:T(8,128)(2,1)}) %all-gather.2.cloned.1.call-update) | async-done | bytes 1048592 | tf_op jit(solution)/shard_map/all_gather | solution.py:12
  41.2 551.5 %while.48 = (s32[]{:T(128)}, bf16[16,2048]{1,0:T(8,128)(2,1)S(1)}, bf16[8,16,2048]{2,1,0:T(8,128)(2,1)S(1)}, bf16[8,32,2048]{2,1,0:T(8,128)(2,1)}, bf16[8,16,1,2...) while((s32[]{:T(128)}, bf16[16,2048]{1,0:T(8,128)(2,1)S(1)}, ...), condition=%wide.region_7.8_spmd, body=%wide.region_0.7_spmd.sunk | while | flops 209598352 | bytes 11630114 | solution.py:164
  45.0 7.0 all-to-all-start
  53.4 6.4 all-to-all-done
  68.5 7.1 all-to-all-done.1
  87.7 6.5 all-to-all-done
  103.0 7.2 all-to-all-done.1
  122.2 6.4 all-to-all-done
  137.3 7.0 all-to-all-done.1
  158.6 6.4 all-to-all-done
  173.7 7.0 all-to-all-done.1
  195.5 6.4 all-to-all-done
  210.6 7.0 all-to-all-done.1
  232.4 6.4 all-to-all-done
  247.5 7.1 all-to-all-done.1
  269.3 6.4 all-to-all-done
  284.4 7.0 all-to-all-done.1
  306.2 6.4 all-to-all-done
  321.3 7.0 all-to-all-done.1
  343.1 6.4 all-to-all-done
  358.2 7.0 all-to-all-done.1
  380.0 6.4 all-to-all-done
  395.1 7.0 all-to-all-done.1
  416.9 6.4 all-to-all-done
  432.0 7.0 all-to-all-done.1
  453.8 6.4 all-to-all-done
  469.0 7.0 all-to-all-done.1
  490.7 6.4 all-to-all-done
  505.9 7.0 all-to-all-done.1
  527.7 6.4 all-to-all-done
  542.8 7.0 all-to-all-done.1
  564.6 6.4 all-to-all-done
  579.7 7.0 all-to-all-done.1
  596.8 642.6 %while.49 = (s32[]{:T(128)}, bf16[16,2048]{1,0:T(8,128)(2,1)S(1)}, bf16[8,16,1,2,2048]{4,3,1,2,0:T(2,128)(2,1)}, bf16[8,16,1,2,512]{4,1,3,2,0:T(8,128)(2,1)}, bf...) while((s32[]{:T(128)}, bf16[16,2048]{1,0:T(8,128)(2,1)S(1)}, ...), condition=%wide.region_18.19_spmd.clone, body=%wide.region_8.18_spmd.clone.sunk | while | flops 351425984 | bytes 17749480 | solution.py:234
  618.8 7.2 all-to-all-start.3
  628.2 5.6 all-to-all-done.3
  662.4 7.2 all-to-all-start.3
  671.8 5.6 all-to-all-done.3
  706.6 7.1 all-to-all-start.3
  716.0 5.6 all-to-all-done.3
  749.0 7.1 all-to-all-start.3
  758.4 5.6 all-to-all-done.3
  791.7 7.1 all-to-all-start.3
  801.1 5.6 all-to-all-done.3
  834.4 7.1 all-to-all-start.3
  843.8 5.6 all-to-all-done.3
  877.1 7.1 all-to-all-start.3
  886.5 5.6 all-to-all-done.3
  919.8 7.1 all-to-all-start.3
  929.2 5.6 all-to-all-done.3
  962.5 7.1 all-to-all-start.3
  971.9 5.6 all-to-all-done.3
  1005.2 7.1 all-to-all-start.3
  1014.6 5.6 all-to-all-done.3
  1047.9 7.1 all-to-all-start.3
  1057.3 5.6 all-to-all-done.3
  1090.6 7.1 all-to-all-start.3
  1133.3 7.1 all-to-all-start.3
  1142.7 5.6 all-to-all-done.3
  1176.0 7.1 all-to-all-start.3
  1185.4 5.6 all-to-all-done.3
  1218.7 7.1 all-to-all-start.3
  1253.0 6.7 all-to-all-start.4
  1280.1 12.3 all-to-all-done.5
  (1339 shorter events, 847.3 us)
Async XLA Ops:
  7.2 28.8 %all-gather.2.cloned.1.call-start = ((), (), s32[]{:S(2)}) async-start(), calls=%async_computation.7 | async-start | bytes 1179648 | tf_op jit(solution)/shard_map/all_gather | solution.py:12
  45.0 14.8 %all-to-all-start = ((bf16[16,1,2,2048]{3,2,1,0:T(2,128)(2,1)}), bf16[16,1,2,2048]{3,2,1,0:T(2,128)(2,1)S(1)}, u32[]{:S(2)}, u32[]{:S(2)}) async-start(bf16[16,1,2,2048]{3,2,1,0:T(2,128)(2,1)} %bitcast.333), calls=%async_computation | async-start | bytes 262144 | tf_op jit(solution)/shard_map/while/body/eval_jaxpr/all_to_all | solution.py:142
  64.1 11.4 all-to-all-start.1
  82.7 11.5 all-to-all-start
  98.4 11.7 all-to-all-start.1
  117.2 11.3 all-to-all-start
  132.8 11.4 all-to-all-start.1
  153.5 11.5 all-to-all-start
  169.3 11.4 all-to-all-start.1
  190.4 11.5 all-to-all-start
  206.2 11.4 all-to-all-start.1
  227.3 11.5 all-to-all-start
  243.1 11.4 all-to-all-start.1
  264.2 11.5 all-to-all-start
  280.0 11.4 all-to-all-start.1
  301.2 11.5 all-to-all-start
  316.9 11.4 all-to-all-start.1
  338.1 11.5 all-to-all-start
  353.8 11.4 all-to-all-start.1
  375.0 11.5 all-to-all-start
  390.7 11.4 all-to-all-start.1
  411.9 11.5 all-to-all-start
  427.6 11.4 all-to-all-start.1
  448.8 11.5 all-to-all-start
  464.5 11.4 all-to-all-start.1
  485.7 11.5 all-to-all-start
  501.4 11.4 all-to-all-start.1
  522.6 11.5 all-to-all-start
  538.4 11.4 all-to-all-start.1
  559.5 11.5 all-to-all-start
  575.3 11.4 all-to-all-start.1
  602.2 11.5 all-to-all-start.2
  618.8 15.0 %all-to-all-start.3 = ((bf16[16,1,2,2048]{3,2,1,0:T(2,128)(2,1)}), bf16[16,1,2,2048]{3,2,1,0:T(2,128)(2,1)S(1)}, u32[]{:S(2)}, u32[]{:S(2)}) async-start(bf16[16,1,2,2048]{3,2,1,0:T(2,128)(2,1)} %copy.132), calls=%async_computation.3 | async-start | bytes 262144 | tf_op jit(solution)/shard_map/while/body/eval_jaxpr/all_to_all | solution.py:191
  645.8 11.4 all-to-all-start.2
  662.4 15.0 %all-to-all-start.3 = ((bf16[16,1,2,2048]{3,2,1,0:T(2,128)(2,1)}), bf16[16,1,2,2048]{3,2,1,0:T(2,128)(2,1)S(1)}, u32[]{:S(2)}, u32[]{:S(2)}) async-start(bf16[16,1,2,2048]{3,2,1,0:T(2,128)(2,1)} %copy.132), calls=%async_computation.3 | async-start | bytes 262144 | tf_op jit(solution)/shard_map/while/body/eval_jaxpr/all_to_all | solution.py:191
  690.0 11.5 all-to-all-start.2
  706.6 14.9 %all-to-all-start.3 = ((bf16[16,1,2,2048]{3,2,1,0:T(2,128)(2,1)}), bf16[16,1,2,2048]{3,2,1,0:T(2,128)(2,1)S(1)}, u32[]{:S(2)}, u32[]{:S(2)}) async-start(bf16[16,1,2,2048]{3,2,1,0:T(2,128)(2,1)} %copy.132), calls=%async_computation.3 | async-start | bytes 262144 | tf_op jit(solution)/shard_map/while/body/eval_jaxpr/all_to_all | solution.py:191
  732.4 11.5 all-to-all-start.2
  749.0 14.9 %all-to-all-start.3 = ((bf16[16,1,2,2048]{3,2,1,0:T(2,128)(2,1)}), bf16[16,1,2,2048]{3,2,1,0:T(2,128)(2,1)S(1)}, u32[]{:S(2)}, u32[]{:S(2)}) async-start(bf16[16,1,2,2048]{3,2,1,0:T(2,128)(2,1)} %copy.132), calls=%async_computation.3 | async-start | bytes 262144 | tf_op jit(solution)/shard_map/while/body/eval_jaxpr/all_to_all | solution.py:191
  775.1 11.5 all-to-all-start.2
  791.7 14.9 %all-to-all-start.3 = ((bf16[16,1,2,2048]{3,2,1,0:T(2,128)(2,1)}), bf16[16,1,2,2048]{3,2,1,0:T(2,128)(2,1)S(1)}, u32[]{:S(2)}, u32[]{:S(2)}) async-start(bf16[16,1,2,2048]{3,2,1,0:T(2,128)(2,1)} %copy.132), calls=%async_computation.3 | async-start | bytes 262144 | tf_op jit(solution)/shard_map/while/body/eval_jaxpr/all_to_all | solution.py:191
  817.8 11.5 all-to-all-start.2
  834.4 14.9 %all-to-all-start.3 = ((bf16[16,1,2,2048]{3,2,1,0:T(2,128)(2,1)}), bf16[16,1,2,2048]{3,2,1,0:T(2,128)(2,1)S(1)}, u32[]{:S(2)}, u32[]{:S(2)}) async-start(bf16[16,1,2,2048]{3,2,1,0:T(2,128)(2,1)} %copy.132), calls=%async_computation.3 | async-start | bytes 262144 | tf_op jit(solution)/shard_map/while/body/eval_jaxpr/all_to_all | solution.py:191
  860.5 11.5 all-to-all-start.2
  877.1 14.9 %all-to-all-start.3 = ((bf16[16,1,2,2048]{3,2,1,0:T(2,128)(2,1)}), bf16[16,1,2,2048]{3,2,1,0:T(2,128)(2,1)S(1)}, u32[]{:S(2)}, u32[]{:S(2)}) async-start(bf16[16,1,2,2048]{3,2,1,0:T(2,128)(2,1)} %copy.132), calls=%async_computation.3 | async-start | bytes 262144 | tf_op jit(solution)/shard_map/while/body/eval_jaxpr/all_to_all | solution.py:191
  903.2 11.5 all-to-all-start.2
  919.8 14.9 %all-to-all-start.3 = ((bf16[16,1,2,2048]{3,2,1,0:T(2,128)(2,1)}), bf16[16,1,2,2048]{3,2,1,0:T(2,128)(2,1)S(1)}, u32[]{:S(2)}, u32[]{:S(2)}) async-start(bf16[16,1,2,2048]{3,2,1,0:T(2,128)(2,1)} %copy.132), calls=%async_computation.3 | async-start | bytes 262144 | tf_op jit(solution)/shard_map/while/body/eval_jaxpr/all_to_all | solution.py:191
  945.9 11.5 all-to-all-start.2
  962.5 14.9 %all-to-all-start.3 = ((bf16[16,1,2,2048]{3,2,1,0:T(2,128)(2,1)}), bf16[16,1,2,2048]{3,2,1,0:T(2,128)(2,1)S(1)}, u32[]{:S(2)}, u32[]{:S(2)}) async-start(bf16[16,1,2,2048]{3,2,1,0:T(2,128)(2,1)} %copy.132), calls=%async_computation.3 | async-start | bytes 262144 | tf_op jit(solution)/shard_map/while/body/eval_jaxpr/all_to_all | solution.py:191
  988.6 11.5 all-to-all-start.2
  1005.2 15.0 %all-to-all-start.3 = ((bf16[16,1,2,2048]{3,2,1,0:T(2,128)(2,1)}), bf16[16,1,2,2048]{3,2,1,0:T(2,128)(2,1)S(1)}, u32[]{:S(2)}, u32[]{:S(2)}) async-start(bf16[16,1,2,2048]{3,2,1,0:T(2,128)(2,1)} %copy.132), calls=%async_computation.3 | async-start | bytes 262144 | tf_op jit(solution)/shard_map/while/body/eval_jaxpr/all_to_all | solution.py:191
  1031.3 11.5 all-to-all-start.2
  1047.9 14.9 %all-to-all-start.3 = ((bf16[16,1,2,2048]{3,2,1,0:T(2,128)(2,1)}), bf16[16,1,2,2048]{3,2,1,0:T(2,128)(2,1)S(1)}, u32[]{:S(2)}, u32[]{:S(2)}) async-start(bf16[16,1,2,2048]{3,2,1,0:T(2,128)(2,1)} %copy.132), calls=%async_computation.3 | async-start | bytes 262144 | tf_op jit(solution)/shard_map/while/body/eval_jaxpr/all_to_all | solution.py:191
  1074.0 11.5 all-to-all-start.2
  1090.6 14.9 %all-to-all-start.3 = ((bf16[16,1,2,2048]{3,2,1,0:T(2,128)(2,1)}), bf16[16,1,2,2048]{3,2,1,0:T(2,128)(2,1)S(1)}, u32[]{:S(2)}, u32[]{:S(2)}) async-start(bf16[16,1,2,2048]{3,2,1,0:T(2,128)(2,1)} %copy.132), calls=%async_computation.3 | async-start | bytes 262144 | tf_op jit(solution)/shard_map/while/body/eval_jaxpr/all_to_all | solution.py:191
  1116.7 11.5 all-to-all-start.2
  1133.3 14.9 %all-to-all-start.3 = ((bf16[16,1,2,2048]{3,2,1,0:T(2,128)(2,1)}), bf16[16,1,2,2048]{3,2,1,0:T(2,128)(2,1)S(1)}, u32[]{:S(2)}, u32[]{:S(2)}) async-start(bf16[16,1,2,2048]{3,2,1,0:T(2,128)(2,1)} %copy.132), calls=%async_computation.3 | async-start | bytes 262144 | tf_op jit(solution)/shard_map/while/body/eval_jaxpr/all_to_all | solution.py:191
  1159.4 11.5 all-to-all-start.2
  1176.0 15.0 %all-to-all-start.3 = ((bf16[16,1,2,2048]{3,2,1,0:T(2,128)(2,1)}), bf16[16,1,2,2048]{3,2,1,0:T(2,128)(2,1)S(1)}, u32[]{:S(2)}, u32[]{:S(2)}) async-start(bf16[16,1,2,2048]{3,2,1,0:T(2,128)(2,1)} %copy.132), calls=%async_computation.3 | async-start | bytes 262144 | tf_op jit(solution)/shard_map/while/body/eval_jaxpr/all_to_all | solution.py:191
  1202.1 11.5 all-to-all-start.2
  1218.7 14.9 %all-to-all-start.3 = ((bf16[16,1,2,2048]{3,2,1,0:T(2,128)(2,1)}), bf16[16,1,2,2048]{3,2,1,0:T(2,128)(2,1)S(1)}, u32[]{:S(2)}, u32[]{:S(2)}) async-start(bf16[16,1,2,2048]{3,2,1,0:T(2,128)(2,1)} %copy.132), calls=%async_computation.3 | async-start | bytes 262144 | tf_op jit(solution)/shard_map/while/body/eval_jaxpr/all_to_all | solution.py:191
  1241.7 11.3 all-to-all-start.6
  1253.0 17.0 %all-to-all-start.4 = ((bf16[8,8,16,256]{3,2,1,0:T(8,128)(2,1)}), bf16[8,8,16,256]{3,2,1,0:T(8,128)(2,1)S(1)}, u32[]{:S(2)}, u32[]{:S(2)}) async-start(bf16[8,8,16,256]{3,2,1,0:T(8,128)(2,1)} %copy.92), calls=%async_computation.4 | async-start | bytes 1048576 | tf_op jit(solution)/shard_map/all_to_all | solution.py:38
  1271.0 21.3 %all-to-all-start.5 = ((bf16[16,2048,16]{1,2,0:T(8,128)(2,1)}), bf16[16,2048,16]{1,2,0:T(8,128)(2,1)S(1)}, u32[]{:S(2)}, u32[]{:S(2)}) async-start(bf16[16,2048,16]{1,2,0:T(8,128)(2,1)} %broadcast_in_dim.180), calls=%async_computation.5 | async-start | bytes 2097152 | tf_op jit(solution)/shard_map/all_to_all | solution.py:24
  (156 other events, 2171.2 us)
Sparse Core Ops, SparseCore 0:
  10.3 25.7 all-gather.1
where the time goes:
time: 1310 us; the launch traced here: 1300 us
  waiting for transfers between devices  387 us (30%)
  starting transfers between devices  358 us (27%)
  matrix products  217 us (17%)
  other arithmetic  167 us (13%)
  local copies, waits for them, and re-layouts  152 us (12%)
  between operations  14.2 us (1%)
    all_to_all x15, starting transfers between devices, backward_tick(): lax.all_to_all(rows_grad, ('expert', 'dp'), split_axis=0, concat_axis=0,...  107 us
    all_to_all x15, waiting for transfers between devices, expert_forward(): lax.all_to_all(out_rows, ('expert', 'dp'), split_axis=0, concat_axis=0, t...  106 us
    dynamic_update_slice x105, other arithmetic, keep_row(): lax.dynamic_update_index_in_dim(stash, jnp.where(active, value, old_row),...  104 us
    all_to_all x15, waiting for transfers between devices, forward_tick(): lax.all_to_all(send_rows, ('expert', 'dp'), split_axis=0, concat_axis=0,...  96.6 us
    dot_general x30, matrix products, expert_inner(): jnp.einsum('sekd,edf->sekf', exp_rows, w_gu, preferred_element_type=jnp.f...  90.3 us
    all_to_all x15, waiting for transfers between devices, backward_tick(): lax.all_to_all(rows_grad, ('expert', 'dp'), split_axis=0, concat_axis=0,...  83.5 us
    ppermute x30, starting transfers between devices, shifted(): lax.ppermute(value, axis, [(source, source + steps) for source in range(l...  71.8 us
    all_to_all x15, starting transfers between devices, forward_tick(): lax.all_to_all(send_rows, ('expert', 'dp'), split_axis=0, concat_axis=0,...  57.7 us
  transfers between devices with their start and end apart: 94, of which 79 were waited for; matrix products, arithmetic and copies ran while one was open for 17% of the time, Pallas kernels for 0%

commit v1 on v0

v1 whole, which is shorter than its diff:
```python
import functools

import jax
import jax.numpy as jnp
from jax import lax
from jax.experimental import pallas as pl
from jax.experimental.pallas import tpu as pltpu
from jax.sharding import PartitionSpec as P

EPS = 1e-05
GROUP = 1
LAG_E = 1
LAG_R = 3
BACK_E = 1
BACK_R = 3
LANES = 128
MESH = pl.DeviceIdType.MESH
F32 = jnp.float32
BF16 = jnp.bfloat16


def dot(lhs, rhs):
    return jnp.dot(lhs, rhs, preferred_element_type=F32)


def dot_nt(lhs, rhs):
    return lax.dot_general(lhs, rhs, (((1,), (1,)), ((), ())), preferred_element_type=F32)


def dot_tn(lhs, rhs):
    return lax.dot_general(lhs, rhs, (((0,), (0,)), ((), ())), preferred_element_type=F32)


def stack_kernel(
    sizes,
    x_ref, cot_ref, sel_ref, selt_ref, sign_ref, gain_ref, router_ref, wgu_ref, wdn_ref,
    rows_ref, q_ref, hid_ref, dyr_ref, gin_ref, red_ref,
    h_buf, g_buf, u_buf, hs_buf, gs_buf,
    xs_buf, xr_buf, ys_buf, yr_buf, ds_buf, dr_buf, us_buf, ur_buf,
    pick_buf, gate_buf, slope_buf, silu_buf, dul_buf, wide,
    acc_r, acc_g, red_s, red_r, gin_r,
    send_sem, recv_sem, line_send, line_recv, gather_send, gather_recv, gin_send, gin_recv, red_send, red_recv,
):
    ns, ny, nz, cap = sizes
    ne = ny * nz
    micro, tok, width = h_buf.shape
    part = width // ns
    cells = ne * cap
    blk = cap * (width // (2 * LANES))
    folds = width // (2 * LANES)
    group = GROUP
    chunks = micro // group
    ffw = wdn_ref.shape[0]
    sec = lax.axis_index("section")
    ey = lax.axis_index("expert")
    ez = lax.axis_index("dp")

    def ahead(k):
        return {"expert": lax.rem(ey + k // nz, ny), "dp": lax.rem(ez + k % nz, nz)}

    def behind(k):
        return {"expert": lax.rem(ey + ny - k // nz, ny), "dp": lax.rem(ez + nz - k % nz, nz)}

    def far(k):
        ky, kz = k // nz, k % nz
        return min(ky, ny - ky) + min(kz, nz - kz)

    order = sorted(range(1, ne), key=lambda k: -far(k))

    barrier = pltpu.get_barrier_semaphore()
    for k in range(1, ne):
        pl.semaphore_signal(barrier, inc=1, device_id=ahead(k), device_id_type=MESH)
    for step in range(1, ns):
        pl.semaphore_signal(
            barrier, inc=1, device_id={"section": lax.rem(sec + step, ns)}, device_id_type=MESH
        )
    pl.semaphore_wait(barrier, ne - 1 + ns - 1)

    my_cols = pl.ds(pl.multiple_of(sec * part, LANES), part)

    def gather_copy(which, src, dst, owner):
        return pltpu.make_async_remote_copy(
            src_ref=src, dst_ref=dst.at[:, :, my_cols],
            send_sem=gather_send.at[which], recv_sem=gather_recv.at[which],
            device_id={"section": owner}, device_id_type=MESH,
        )

    @pl.when(sec != 0)
    def _():
        gather_copy(0, x_ref, h_buf, 0).start()

    @pl.when(sec != ns - 1)
    def _():
        gather_copy(1, cot_ref, g_buf, ns - 1).start()

    @pl.when(sec == 0)
    def _():
        h_buf[:, :, 0:part] = x_ref[...]

    @pl.when(sec == ns - 1)
    def _():
        g_buf[:, :, (ns - 1) * part :] = cot_ref[...]

    acc_r[...] = jnp.zeros_like(acc_r)
    acc_g[...] = jnp.zeros_like(acc_g)

    def span(chunk):
        return pl.ds(chunk * group, group)

    def exchange(kind, chunk, src, dst, target):
        for k in order:
            rows = pl.ds(k * blk, blk)
            pltpu.make_async_remote_copy(
                src_ref=src.at[span(chunk), rows], dst_ref=dst.at[span(chunk), rows],
                send_sem=send_sem.at[kind, chunk], recv_sem=recv_sem.at[kind, chunk],
                device_id=target(k), device_id_type=MESH,
            ).start()

    def arrived(kind, chunk, dst):
        part_ref = dst.at[span(chunk), pl.ds(blk, (ne - 1) * blk)]
        pltpu.make_async_copy(part_ref, part_ref, recv_sem.at[kind, chunk]).wait()

    def fold(value, at, send, recv):
        for j in range(folds):
            for half in range(2):
                left = (2 * j + half) * LANES
                wide[half, pl.ds(j, cells, stride=folds), :] = value[:, left : left + LANES]
        for half in range(2):
            cols = slice(half * LANES, (half + 1) * LANES)
            packed = wide[half].astype(BF16)
            send[at, :, cols] = packed
            recv[at, 0:blk, cols] = packed[0:blk]

    def unfold(at, recv):
        for half in range(2):
            wide[half] = recv[at, :, half * LANES : (half + 1) * LANES].astype(F32)
        pieces = [
            wide[half, pl.ds(j, cells, stride=folds), :] for j in range(folds) for half in range(2)
        ]
        return jnp.concatenate(pieces, axis=1).astype(BF16)

    def line_copy(way, chunk, src, dst, target):
        return pltpu.make_async_remote_copy(
            src_ref=src.at[span(chunk)], dst_ref=dst.at[span(chunk)],
            send_sem=line_send.at[way, chunk], recv_sem=line_recv.at[way, chunk],
            device_id={"section": target}, device_id_type=MESH,
        )

    def inv_rms(h_wide):
        return lax.rsqrt(jnp.mean(h_wide * h_wide, axis=-1, keepdims=True) + EPS)

    def wait_gather(which, dst):
        part_ref = dst.at[:, :, pl.ds(0, (ns - 1) * part)]
        pltpu.make_async_copy(part_ref, part_ref, gather_recv.at[which]).wait()

    def tokens_out(chunk):
        @pl.when((sec == 0) & (chunk == 0))
        def _():
            wait_gather(0, h_buf)

        @pl.when(sec != 0)
        def _():
            line_copy(0, chunk, hs_buf, h_buf, 0).wait_recv()

        for n in range(group):
            at = chunk * group + n
            h_wide = h_buf[at].astype(F32)
            normed = (h_wide * inv_rms(h_wide) * gain_ref[...]).astype(BF16)
            u_buf[at] = normed
            both = jnp.concatenate([normed, normed], axis=0)
            fold(dot(selt_ref[at], both), at, xs_buf, xr_buf)
        exchange(0, chunk, xs_buf, xr_buf, ahead)
        for n in range(group):
            at = chunk * group + n
            logits = dot_nt(u_buf[at], router_ref[...])
            gap = jnp.sum(logits * sign_ref[at], axis=-1, keepdims=True)
            gates = jnp.concatenate([jax.nn.sigmoid(gap), jax.nn.sigmoid(-gap)], axis=0)
            gate_buf[at] = jnp.broadcast_to(gates, (2 * tok, LANES))

    def experts(chunk):
        arrived(0, chunk, xr_buf)
        rows = pl.ds(pl.multiple_of(chunk * group * cells, cells), group * cells)
        for n in range(group):
            at = chunk * group + n
            rows_ref[pl.ds(pl.multiple_of(at * cells, cells), cells), :] = unfold(at, xr_buf)
        gate_up = dot(rows_ref[rows, :], wgu_ref[...])
        gate_part = gate_up[:, :ffw]
        up_part = gate_up[:, ffw:]
        sig = jax.nn.sigmoid(gate_part)
        silu = gate_part * sig
        hidden = (silu * up_part).astype(BF16)
        hid_ref[rows, :] = hidden
        out = dot(hidden, wdn_ref[...])
        for n in range(group):
            fold(out[n * cells : (n + 1) * cells], chunk * group + n, ys_buf, yr_buf)
        exchange(1, chunk, ys_buf, yr_buf, behind)
        silu_buf[rows, :] = silu
        slope_buf[rows, :] = up_part * (sig * (1.0 + gate_part * (1.0 - sig)))

    def tokens_in(chunk):
        arrived(1, chunk, yr_buf)
        for n in range(group):
            at = chunk * group + n
            picked = dot(sel_ref[at], unfold(at, yr_buf))
            pick_buf[at] = picked.astype(BF16)
            gates = gate_buf[at][:, :1]
            total = h_buf[at].astype(F32) + gates[:tok] * picked[:tok] + gates[tok:] * picked[tok:]
            hs_buf[at] = total.astype(BF16)

        @pl.when(sec != ns - 1)
        def _():
            line_copy(0, chunk, hs_buf, h_buf, sec + 1).start()

    def schedule(first, second, third, lag_second, lag_third):
        def step(i, carry):
            @pl.when(i < chunks)
            def _():
                first(i)

            @pl.when((i >= lag_second) & (i < chunks + lag_second))
            def _():
                second(i - lag_second)

            @pl.when(i >= lag_third)
            def _():
                third(i - lag_third)

            return carry

        lax.fori_loop(0, chunks + lag_third, step, 0)

    schedule(tokens_out, experts, tokens_in, LAG_E, LAG_R)

    def grads_out(chunk):
        @pl.when((sec == ns - 1) & (chunk == 0))
        def _():
            wait_gather(1, g_buf)

        @pl.when(sec != ns - 1)
        def _():
            line_copy(1, chunk, gs_buf, g_buf, 0).wait_recv()

        for n in range(group):
            at = chunk * group + n
            grad = g_buf[at].astype(F32)
            gates = gate_buf[at][:, :1]
            scaled = (jnp.concatenate([grad, grad], axis=0) * gates).astype(BF16)
            fold(dot(selt_ref[at], scaled), at, ds_buf, dr_buf)
        exchange(2, chunk, ds_buf, dr_buf, ahead)
        for n in range(group):
            at = chunk * group + n
            grad = g_buf[at].astype(F32)
            gates = gate_buf[at][:, :1]
            picked = pick_buf[at].astype(F32)
            diff = jnp.sum(grad * (picked[:tok] - picked[tok:]), axis=-1, keepdims=True)
            cols = (gates[:tok] * gates[tok:] * diff * sign_ref[at]).astype(BF16)
            dul_buf[at] = dot(cols, router_ref[...])
            acc_r[...] += dot_tn(cols, u_buf[at])

    def expert_grads(chunk):
        arrived(2, chunk, dr_buf)
        rows = pl.ds(pl.multiple_of(chunk * group * cells, cells), group * cells)
        for n in range(group):
            at = chunk * group + n
            dyr_ref[pl.ds(pl.multiple_of(at * cells, cells), cells), :] = unfold(at, dr_buf)
        d_hidden = dot_nt(dyr_ref[rows, :], wdn_ref[...])
        q_ref[rows, :ffw] = (d_hidden * slope_buf[rows, :]).astype(BF16)
        q_ref[rows, ffw:] = (d_hidden * silu_buf[rows, :]).astype(BF16)
        out = dot_nt(q_ref[rows, :], wgu_ref[...])
        for n in range(group):
            fold(out[n * cells : (n + 1) * cells], chunk * group + n, us_buf, ur_buf)
        exchange(3, chunk, us_buf, ur_buf, behind)

    def gin_copy(chunk, target):
        return pltpu.make_async_remote_copy(
            src_ref=gs_buf.at[span(chunk), :, pl.ds(target * part, part)],
            dst_ref=gin_r.at[span(chunk)],
            send_sem=gin_send.at[target, chunk], recv_sem=gin_recv.at[chunk],
            device_id={"section": target}, device_id_type=MESH,
        )

    def grads_in(chunk):
        arrived(3, chunk, ur_buf)
        for n in range(group):
            at = chunk * group + n
            picked = dot(sel_ref[at], unfold(at, ur_buf))
            grad_u = picked[:tok] + picked[tok:] + dul_buf[at]
            h_wide = h_buf[at].astype(F32)
            inv = inv_rms(h_wide)
            scaled = grad_u * gain_ref[...]
            proj = jnp.mean(scaled * h_wide, axis=-1, keepdims=True)
            grad = g_buf[at].astype(F32) + inv * scaled - h_wide * (inv * inv * inv * proj)
            gs_buf[at] = grad.astype(BF16)

        @pl.when(sec != 0)
        def _():
            line_copy(1, chunk, gs_buf, g_buf, sec - 1).start()

        @pl.when(sec == 0)
        def _():
            for target in range(1, ns):
                gin_copy(chunk, target).start()
            gin_ref[span(chunk)] = gs_buf[span(chunk), :, 0:part]

        for n in range(group):
            at = chunk * group + n
            picked = dot(sel_ref[at], unfold(at, ur_buf))
            grad_u = picked[:tok] + picked[tok:] + dul_buf[at]
            h_wide = h_buf[at].astype(F32)
            acc_g[...] += jnp.sum(grad_u * h_wide * inv_rms(h_wide), axis=0, keepdims=True)

    schedule(grads_out, expert_grads, grads_in, BACK_E, BACK_R)

    red_s[:, :width] = acc_r[...].astype(BF16)
    per = width // ne
    gains = [acc_g[:, i * per : (i + 1) * per] for i in range(ne)]
    red_s[:, width:] = jnp.concatenate(gains, axis=0).astype(BF16)

    def red_copy(k):
        return pltpu.make_async_remote_copy(
            src_ref=red_s, dst_ref=red_r.at[k],
            send_sem=red_send, recv_sem=red_recv,
            device_id=ahead(k), device_id_type=MESH,
        )

    for k in order:
        red_copy(k).start()

    @pl.when(sec != 0)
    def _():
        def take(chunk, carry):
            dst = gin_r.at[span(chunk)]
            pltpu.make_async_copy(dst, dst, gin_recv.at[chunk]).wait()
            return carry

        lax.fori_loop(0, chunks, take, 0)
        gin_ref[...] = gin_r[...]

    others = red_r.at[pl.ds(1, ne - 1)]
    pltpu.make_async_copy(others, others, red_recv).wait()
    total = red_s[...].astype(F32)
    for k in range(1, ne):
        total = total + red_r[k].astype(F32)
    red_ref[...] = total

    pltpu.make_async_copy(others, others, red_send).wait()

    def drain(chunk, carry):
        for kind, buf in enumerate((xs_buf, ys_buf, ds_buf, us_buf)):
            part_ref = buf.at[span(chunk), pl.ds(blk, (ne - 1) * blk)]
            pltpu.make_async_copy(part_ref, part_ref, send_sem.at[kind, chunk]).wait()

        @pl.when(sec != ns - 1)
        def _():
            line_copy(0, chunk, hs_buf, h_buf, 0).wait_send()

        @pl.when(sec != 0)
        def _():
            line_copy(1, chunk, gs_buf, g_buf, 0).wait_send()

        @pl.when(sec == 0)
        def _():
            for target in range(1, ns):
                gin_copy(chunk, target).wait_send()

        return carry

    lax.fori_loop(0, chunks, drain, 0)

    @pl.when(sec != 0)
    def _():
        gather_copy(0, x_ref, h_buf, 0).wait_send()

    @pl.when(sec != ns - 1)
    def _():
        gather_copy(1, cot_ref, g_buf, ns - 1).wait_send()


def slot_tables(route_rows, n_expert, capacity, ny, nz):
    micro, tok, _ = route_rows.shape
    ey, ez = lax.axis_index("expert"), lax.axis_index("dp")
    named = jnp.transpose(route_rows, (0, 2, 1)).reshape(micro, 2 * tok)
    token = jnp.arange(2 * tok, dtype=jnp.int32) % tok
    same = (named[:, :, None] == named[:, None, :]) & (token[None, :] < token[:, None])
    slot = jnp.sum(same.astype(jnp.int32), axis=2)
    rel = ((named // nz - ey) % ny) * nz + (named % nz - ez) % nz
    cell = rel * capacity + slot
    ids = jnp.arange(n_expert * capacity, dtype=jnp.int32)
    sel = (cell[:, :, None] == ids).astype(BF16)
    selt = (cell[:, None, :] == ids[:, None]).astype(BF16)
    experts = jnp.arange(n_expert, dtype=jnp.int32)
    hits = (named[:, :, None] == experts).astype(F32)
    sign = hits[:, :tok] - hits[:, tok:]
    return sel, selt, sign


def local(x_in, cotangent, route_ids, norm_gain, router, w_gate_up, w_down):
    ns, ny, nz = (lax.axis_size(a) for a in ("section", "expert", "dp"))
    micro, tok, part = x_in.shape
    width = part * ns
    ne = ny * nz
    cap = 2 * tok // ne
    cells = ne * cap
    ffw = w_down.shape[2]
    chunks = micro // GROUP
    sel, selt, sign = slot_tables(route_ids[0], ne, cap, ny, nz)
    wire = pltpu.VMEM((micro, cells * width // (2 * LANES), 2 * LANES), BF16)
    rows = pltpu.VMEM((micro, tok, width), BF16)
    dma = pltpu.SemaphoreType.DMA
    red_width = width + width // ne
    scratch = (
        [rows] * 5
        + [wire] * 8
        + [
            pltpu.VMEM((micro, 2 * tok, width), BF16),
            pltpu.VMEM((micro, 2 * tok, LANES), F32),
            pltpu.VMEM((micro * cells, ffw), F32),
            pltpu.VMEM((micro * cells, ffw), F32),
            pltpu.VMEM((micro, tok, width), F32),
            pltpu.VMEM((2, cells * width // (2 * LANES), LANES), F32),
            pltpu.VMEM((ne, width), F32),
            pltpu.VMEM((1, width), F32),
            pltpu.VMEM((ne, red_width), BF16),
            pltpu.VMEM((ne, ne, red_width), BF16),
            pltpu.VMEM((micro, tok, part), BF16),
            dma((4, chunks)), dma((4, chunks)), dma((2, chunks)), dma((2, chunks)),
            dma((2,)), dma((2,)), dma((ns, chunks)), dma((chunks,)), dma, dma,
        ]
    )
    outs = (
        jax.ShapeDtypeStruct((micro * cells, width), BF16),
        jax.ShapeDtypeStruct((micro * cells, 2 * ffw), BF16),
        jax.ShapeDtypeStruct((micro * cells, ffw), BF16),
        jax.ShapeDtypeStruct((micro * cells, width), BF16),
        jax.ShapeDtypeStruct((micro, tok, part), BF16),
        jax.ShapeDtypeStruct((ne, red_width), F32),
    )
    exp_rows, q, hidden, dy_rows, grad_in, red = pl.pallas_call(
        functools.partial(stack_kernel, (ns, ny, nz, cap)),
        out_shape=outs,
        in_specs=[pl.BlockSpec(memory_space=pltpu.VMEM)] * 9,
        out_specs=[pl.BlockSpec(memory_space=pltpu.VMEM)] * 6,
        scratch_shapes=scratch,
        compiler_params=pltpu.CompilerParams(
            collective_id=0, has_side_effects=True, vmem_limit_bytes=60 * 1024 * 1024
        ),
    )(
        x_in, cotangent, sel, selt, sign, norm_gain, router[0].T,
        w_gate_up[0, 0], w_down[0, 0],
    )
    grad_gu = dot_tn(exp_rows, q)
    grad_dn = dot_tn(hidden, dy_rows)
    sum_router = red[:, :width].T
    sum_gain = red[:, width:].reshape(width)
    return grad_in, grad_gu[None, None], grad_dn[None, None], sum_router[None], sum_gain[None]


def solution(mesh):
    in_specs = (
        P(None, ("expert", "dp"), "section"),
        P(None, ("expert", "dp"), "section"),
        P("section", None, ("expert", "dp"), None),
        P("section", None),
        P("section", None, None),
        P("section", ("expert", "dp"), None, None),
        P("section", ("expert", "dp"), None, None),
    )
    out_specs = (
        P(None, ("expert", "dp"), "section"),
        P("section", ("expert", "dp"), None, None),
        P("section", ("expert", "dp"), None, None),
        P("section", None, None),
        P("section", None),
    )
    return jax.shard_map(local, mesh=mesh, in_specs=in_specs, out_specs=out_specs, check_vma=False)
```

time: 1310 us -> 352 us (0.27)
  waiting for transfers between devices: 387 us -> 0 us
  starting transfers between devices: 358 us -> 0 us
  Pallas kernels: 0 us -> 338 us
  matrix products: 217 us -> 8.89 us
  other arithmetic: 167 us -> 1.87 us
  local copies, waits for them, and re-layouts: 152 us -> 2.68 us
  between operations: 14.2 us -> 0.68 us
    pallas_call x0 -> x1, Pallas kernels: none -> 338 us  [local(): pl.pallas_call(functools.partial(stack_kernel, (ns, ny, nz, cap)), out_sh...]
    all_to_all x63 -> x0, waiting for transfers between devices: 311 us -> none  [the longest x15 106 us: expert_forward(): lax.all_to_all(out_rows, ('expert', 'dp'), split_axis=0, concat_axis=0, t...]
    all_to_all x63 -> x0, starting transfers between devices: 286 us -> none  [the longest x15 107 us: backward_tick(): lax.all_to_all(rows_grad, ('expert', 'dp'), split_axis=0, concat_axis=0,...]
    dot_general x212 -> x2, matrix products: 217 us -> 8.89 us  [dot_tn(): lax.dot_general(lhs, rhs, (((0,), (0,)), ((), ())), preferred_element_typ...]
    dynamic_update_slice x105 -> x0, other arithmetic: 104 us -> none  [keep_row(): lax.dynamic_update_index_in_dim(stash, jnp.where(active, value, old_row),...]
    ppermute x30 -> x0, starting transfers between devices: 71.8 us -> none  [shifted(): lax.ppermute(value, axis, [(source, source + steps) for source in range(l...]
    dynamic_slice x90 -> x0, local copies, waits for them, and re-layouts: 69.4 us -> none  [the longest x75 54.5 us: keep_row(): old_row = lax.dynamic_index_in_dim(stash, position, 0, keepdims=False)]
    ppermute x30 -> x0, waiting for transfers between devices: 48.9 us -> none  [shifted(): lax.ppermute(value, axis, [(source, source + steps) for source in range(l...]
  transfers between devices with their start and end apart: 94 -> 0, of which waited for: 79 -> 0; matrix products, arithmetic and copies ran while one was open for 17% -> 0% of each run, Pallas kernels for 0% -> 0%
where the time goes in v1:
time: 352 us
  Pallas kernels  338 us (96%)
  matrix products  8.89 us (3%)
    pallas_call x1, Pallas kernels, local(): pl.pallas_call(functools.partial(stack_kernel, (ns, ny, nz, cap)), out_sh...  338 us
    dot_general x2, matrix products, dot_tn(): lax.dot_general(lhs, rhs, (((0,), (0,)), ((), ())), preferred_element_typ...  8.89 us

profile of v1, /device:TPU:0, one launch (start us, length us, event | category | flops | bytes accessed | tf_op | source)
XLA Modules:
  0.0 351.6 jit_solution(290215073609312490)
XLA Ops:
  0.6 0.8 reshape.216
  1.4 0.1 broadcast_compare_fusion
  1.5 0.3 convert_reduce_fusion
  1.8 0.7 fusion.1
  2.6 0.1 fusion.2
  2.7 0.6 slice_subtract_fusion.sign_ref
  3.3 337.5 %shard_map.110 = (bf16[256,2048]{1,0:T(8,128)(2,1)}, bf16[256,1024]{1,0:T(8,128)(2,1)}, bf16[256,512]{1,0:T(8,128)(2,1)}, bf16[256,2048]{1,0:T(8,128)(2,1)}, bf1...) custom-call(bf16[8,16,256]{2,1,0:T(8,128)(2,1)} %x_ref.1, bf16[8,16,256]{2,1,0:T(8,128)(2,1)} %cot_ref.1, ...), custom_call_target="tpu_custom_call" | custom-call | tf_op jit(solution)/shard_map/pallas_call | solution.py:438
  340.8 0.0 copy-start
  340.8 0.0 copy-start.1
  340.8 6.1 %convolution_bitcast_fusion = f32[1,1,2048,1024]{3,2,1,0:T(8,128)} fusion(bf16[256,2048]{1,0:T(8,128)(2,1)} %get-tuple-element.12, bf16[256,1024]{1,0:T(8,128)(2,1)} %get-tuple-element.13), kind=kOutput, calls=%fused_computation | convolution fusion | flops 1073741824 | bytes 9961472 | tf_op jit(solution)/shard_map/dot_general | solution.py:31
  347.0 0.0 copy-start.2
  347.0 0.0 copy-start.3
  347.0 0.0 copy-done
  347.0 0.0 copy-done.1
  347.0 2.7 convolution_bitcast_fusion.1
  349.8 0.0 copy-done.2
  349.8 0.7 slice_bitcast_fusion
  350.4 0.6 slice.15
  351.0 0.0 copy-done.3
  351.0 0.6 copy.13
  (2 shorter events, 0.0 us)
Async XLA Ops:
  340.8 6.2 %copy-start = (bf16[256,2048]{1,0:T(8,128)(2,1)S(1)}, bf16[256,2048]{1,0:T(8,128)(2,1)}, u32[]{:S(2)}) copy-start(bf16[256,2048]{1,0:T(8,128)(2,1)} %get-tuple-element.15) | copy-start | bytes 3145732
  340.8 6.2 %copy-start.1 = (bf16[256,512]{1,0:T(8,128)(2,1)S(1)}, bf16[256,512]{1,0:T(8,128)(2,1)}, u32[]{:S(2)}) copy-start(bf16[256,512]{1,0:T(8,128)(2,1)} %get-tuple-element.14) | copy-start | bytes 786436
  347.0 2.8 copy-start.2
  347.0 4.0 %copy-start.3 = (bf16[8,16,256]{2,1,0:T(8,128)(2,1)S(1)}, bf16[8,16,256]{2,1,0:T(8,128)(2,1)}, u32[]{:S(2)}) copy-start(bf16[8,16,256]{2,1,0:T(8,128)(2,1)} %get-tuple-element.24) | copy-start | bytes 196612

commit v2 on v1

v2 whole, which is shorter than its diff:
```python
import functools

import jax
import jax.numpy as jnp
from jax import lax
from jax.experimental import pallas as pl
from jax.experimental.pallas import tpu as pltpu
from jax.sharding import PartitionSpec as P

EPS = 1e-05
GROUP = 1
LAG = 1
BETWEEN = 5
LANES = 128
MESH = pl.DeviceIdType.MESH
F32 = jnp.float32
BF16 = jnp.bfloat16


def dot(lhs, rhs):
    return jnp.dot(lhs, rhs, preferred_element_type=F32)


def dot_nt(lhs, rhs):
    return lax.dot_general(lhs, rhs, (((1,), (1,)), ((), ())), preferred_element_type=F32)


def dot_tn(lhs, rhs):
    return lax.dot_general(lhs, rhs, (((0,), (0,)), ((), ())), preferred_element_type=F32)


def stack_kernel(
    sizes,
    x_ref, cot_ref, route_ref, gain_ref, router_ref, wgu_hbm, wdn_hbm,
    rows_hbm, q_hbm, hid_hbm, dyr_hbm, gin_ref, router_sum_ref, gain_sum_ref,
    wgu_ref, wdn_ref, rows_ref, q_ref, hid_ref, dyr_ref, tab, tab_in, sign_ref,
    h_buf, hin_buf, g_buf, u_buf, gs_buf,
    xs_buf, xr_buf, ys_buf, yr_buf, yl_buf, ds_buf, dn_buf, dr_buf, us_buf, ur_buf,
    pick_buf, gate_buf, gatein_buf, l_buf, ls_buf, slope_buf, silu_buf, dul_buf, wide,
    acc_r, acc_g, part_s, part_r, sum_s, sum_r, gain_s, gain_r, gin_r,
    send_sem, recv_sem, line_send, line_recv, tab_sem, gather_send, gather_recv, gin_send, gin_recv,
    red_send, red_recv, local_sem,
):
    ns, ny, nz, cap = sizes
    ne = ny * nz
    micro, tok, width = h_buf.shape
    part = width // ns
    cells = ne * cap
    blk = cap * (width // (2 * LANES))
    folds = width // (2 * LANES)
    group = GROUP
    chunks = micro // group
    ffw = wdn_ref.shape[0]
    sec = lax.axis_index("section")
    ey = lax.axis_index("expert")
    ez = lax.axis_index("dp")

    first, last = sec == 0, sec == ns - 1
    inner, lower = sec != ns - 1, sec != 0

    def ahead(k, section=None):
        there = {"expert": lax.rem(ey + k // nz, ny), "dp": lax.rem(ez + k % nz, nz)}
        return there if section is None else {"section": section, **there}

    def behind(k, section=None):
        there = {"expert": lax.rem(ey + ny - k // nz, ny), "dp": lax.rem(ez + nz - k % nz, nz)}
        return there if section is None else {"section": section, **there}

    def far(k):
        ky, kz = k // nz, k % nz
        return min(ky, ny - ky) + min(kz, nz - kz)

    order = sorted(range(1, ne), key=lambda k: -far(k))
    order_all = order + [0]

    loads = [
        pltpu.make_async_copy(src, dst, local_sem.at[n])
        for n, (src, dst) in enumerate(((wgu_hbm, wgu_ref), (wdn_hbm, wdn_ref)))
    ]
    stores = [
        pltpu.make_async_copy(src, dst, local_sem.at[2 + n])
        for n, (src, dst) in enumerate(
            ((rows_ref, rows_hbm), (hid_ref, hid_hbm), (dyr_ref, dyr_hbm), (q_ref, q_hbm))
        )
    ]
    for load in loads:
        load.start()

    barrier = pltpu.get_barrier_semaphore()
    for k in range(1, ne):
        pl.semaphore_signal(barrier, inc=1, device_id=ahead(k), device_id_type=MESH)
        for step in (1, ns - 1):
            there = ahead(k, lax.rem(sec + step, ns))
            pl.semaphore_signal(barrier, inc=1, device_id=there, device_id_type=MESH)
    for step in range(1, ns):
        pl.semaphore_signal(
            barrier, inc=1, device_id={"section": lax.rem(sec + step, ns)}, device_id_type=MESH
        )
    pl.semaphore_wait(barrier, 3 * (ne - 1) + ns - 1)

    my_cols = pl.ds(pl.multiple_of(sec * part, LANES), part)

    def gather_copy(which, src, dst, first, count, owner):
        at = pl.ds(first, count)
        return pltpu.make_async_remote_copy(
            src_ref=src.at[at], dst_ref=dst.at[at, :, my_cols],
            send_sem=gather_send.at[which], recv_sem=gather_recv.at[which],
            device_id={"section": owner}, device_id_type=MESH,
        )

    gathers = (
        gather_copy(0, x_ref, h_buf, 0, group, 0),
        gather_copy(1, x_ref, h_buf, group, micro - group, 0),
        gather_copy(2, cot_ref, g_buf, 0, micro, ns - 1),
    )

    @pl.when(sec != 0)
    def _():
        gathers[0].start()
        gathers[1].start()

    @pl.when(sec != ns - 1)
    def _():
        gathers[2].start()

    @pl.when(sec == 0)
    def _():
        h_buf[:, :, 0:part] = x_ref[...]

    @pl.when(sec == ns - 1)
    def _():
        g_buf[:, :, (ns - 1) * part :] = cot_ref[...]

    kinds = lax.broadcasted_iota(jnp.int32, (ne, tok), 0)
    place = jnp.zeros((ne, tok), F32)
    for e in range(ne):
        rel = lax.rem(e // nz + ny - ey, ny) * nz + lax.rem(e % nz + nz - ez, nz)
        place = jnp.where(kinds == e, (rel * cap).astype(F32), place)
    earlier = lax.broadcasted_iota(jnp.int32, (tok, tok), 0)
    earlier = (earlier < lax.broadcasted_iota(jnp.int32, (tok, tok), 1)).astype(BF16)
    cell_ids = lax.broadcasted_iota(jnp.int32, (cells, tok), 0).astype(F32)

    def eye(n):
        rows_id = lax.broadcasted_iota(jnp.int32, (n, n), 0)
        return (rows_id == lax.broadcasted_iota(jnp.int32, (n, n), 1)).astype(BF16)

    def tables(at, carry):
        named = route_ref[at]
        hits = [(kinds == named[k : k + 1, :]).astype(F32) for k in range(2)]
        before = dot((hits[0] + hits[1]).astype(BF16), earlier) + place
        for k in range(2):
            cell = jnp.sum(hits[k] * before, axis=0, keepdims=True)
            tab[at, 2 * tok :, k * tok : (k + 1) * tok] = (cell_ids == cell).astype(BF16)
        turned = dot_nt(eye(2 * tok), tab[at, 2 * tok :, : 2 * tok])
        tab[at, : 2 * tok, :cells] = turned.astype(BF16)
        sign_ref[at] = dot_nt(eye(tok), (hits[0] - hits[1]).astype(BF16))
        return carry

    tab[...] = jnp.zeros_like(tab)
    lax.fori_loop(0, micro, tables, 0)

    def table_copy(target):
        return pltpu.make_async_remote_copy(
            src_ref=tab, dst_ref=tab_in, send_sem=tab_sem.at[0], recv_sem=tab_sem.at[1],
            device_id={"section": target}, device_id_type=MESH,
        )

    @pl.when(inner)
    def _():
        table_copy(sec + 1).start()

    def pick(table, at):
        return table[at, : 2 * tok, :cells]

    def put(table, at):
        return table[at, 2 * tok :, : 2 * tok]

    acc_r[...] = jnp.zeros_like(acc_r)
    acc_g[...] = jnp.zeros_like(acc_g)

    def span(chunk):
        return pl.ds(chunk * group, group)

    def exchange(sent, kind, chunk, src, dst, target, blocks):
        for k in blocks:
            rows = pl.ds(k * blk, blk)
            pltpu.make_async_remote_copy(
                src_ref=src.at[span(chunk), rows], dst_ref=dst.at[span(chunk), rows],
                send_sem=send_sem.at[sent, chunk], recv_sem=recv_sem.at[kind, chunk],
                device_id=target(k), device_id_type=MESH,
            ).start()

    def wait_all(ref, sem):
        pltpu.make_async_copy(ref, ref, sem).wait()

    def others(buf, chunk):
        return buf.at[span(chunk), pl.ds(blk, (ne - 1) * blk)]

    def arrived(kind, chunk, dst):
        wait_all(others(dst, chunk), recv_sem.at[kind, chunk])

    def all_arrived(kind, chunk, dst):
        wait_all(dst.at[span(chunk)], recv_sem.at[kind, chunk])

    def fold(value, at, send, recv=None):
        for j in range(folds):
            for half in range(2):
                left = (2 * j + half) * LANES
                wide[half, pl.ds(j, cells, stride=folds), :] = value[:, left : left + LANES]
        for half in range(2):
            cols = slice(half * LANES, (half + 1) * LANES)
            packed = wide[half].astype(BF16)
            send[at, :, cols] = packed
            if recv is not None:
                recv[at, 0:blk, cols] = packed[0:blk]

    def unfold(at, recv):
        for half in range(2):
            wide[half] = recv[at, :, half * LANES : (half + 1) * LANES].astype(F32)
        pieces = [
            wide[half, pl.ds(j, cells, stride=folds), :] for j in range(folds) for half in range(2)
        ]
        return jnp.concatenate(pieces, axis=1).astype(BF16)

    def line_copy(way, chunk, src, dst, target):
        return pltpu.make_async_remote_copy(
            src_ref=src.at[span(chunk)], dst_ref=dst.at[span(chunk)],
            send_sem=line_send.at[way, chunk], recv_sem=line_recv.at[way, chunk],
            device_id={"section": target}, device_id_type=MESH,
        )

    def inv_rms(h_wide):
        return lax.rsqrt(jnp.mean(h_wide * h_wide, axis=-1, keepdims=True) + EPS)

    def wait_gather(which, dst, first, count):
        part_ref = dst.at[pl.ds(first, count), :, pl.ds(0, (ns - 1) * part)]
        pltpu.make_async_copy(part_ref, part_ref, gather_recv.at[which]).wait()

    line_h, line_gate, line_g, line_l = range(4)

    def up(way, chunk, target=0):
        pair = (h_buf, hin_buf) if way == line_h else (gate_buf, gatein_buf)
        return line_copy(way, chunk, *pair, target)

    def down(way, chunk, target=0):
        pair = (gs_buf, g_buf) if way == line_g else (ls_buf, l_buf)
        return line_copy(way, chunk, *pair, target)

    def tokens(chunk):
        @pl.when(first & (chunk == 0))
        def _():
            wait_gather(0, h_buf, 0, group)

        @pl.when(first & (chunk == 1))
        def _():
            wait_gather(1, h_buf, group, micro - group)

        @pl.when(lower & (chunk == 0))
        def _():
            table_copy(0).wait_recv()

        @pl.when(lower)
        def _():
            up(line_h, chunk).wait_recv()
            up(line_gate, chunk).wait_recv()
            all_arrived(1, chunk, yr_buf)
            for n in range(group):
                at = chunk * group + n
                picked = dot(pick(tab_in, at), unfold(at, yr_buf))
                gates = gatein_buf[at][:, :1]
                total = gates[:tok] * picked[:tok] + gates[tok:] * picked[tok:]
                h_buf[at] = (hin_buf[at].astype(F32) + total).astype(BF16)
                pick_buf[at] = picked.astype(BF16)

        for n in range(group):
            at = chunk * group + n
            h_wide = h_buf[at].astype(F32)
            normed = (h_wide * inv_rms(h_wide) * gain_ref[...]).astype(BF16)
            u_buf[at] = normed
            both = jnp.concatenate([normed, normed], axis=0)
            fold(dot(put(tab, at), both), at, xs_buf, xr_buf)
        exchange(0, 0, chunk, xs_buf, xr_buf, ahead, order)
        for n in range(group):
            at = chunk * group + n
            logits = dot_nt(u_buf[at], router_ref[...])
            gap = jnp.sum(logits * sign_ref[at], axis=-1, keepdims=True)
            gates = jnp.concatenate([jax.nn.sigmoid(gap), jax.nn.sigmoid(-gap)], axis=0)
            gate_buf[at] = jnp.broadcast_to(gates, (2 * tok, LANES))

        @pl.when(inner)
        def _():
            up(line_h, chunk, sec + 1).start()
            up(line_gate, chunk, sec + 1).start()

        @pl.when(last & (chunk == 0))
        def _():
            wait_gather(2, g_buf, 0, micro)

        @pl.when(last)
        def _():
            for n in range(group):
                at = chunk * group + n
                send_grad(at, g_buf[at].astype(F32), gate_buf, tab, ds_buf, dr_buf)
            exchange(2, 2, chunk, ds_buf, dr_buf, ahead, order)

    def send_grad(at, grad, gate_ref, table, send, recv=None):
        scaled = (jnp.concatenate([grad, grad], axis=0) * gate_ref[at][:, :1]).astype(BF16)
        fold(dot(put(table, at), scaled), at, send, recv)

    def experts(chunk):
        @pl.when(chunk == 0)
        def _():
            for load in loads:
                load.wait()

        arrived(0, chunk, xr_buf)
        rows = pl.ds(pl.multiple_of(chunk * group * cells, cells), group * cells)
        for n in range(group):
            at = chunk * group + n
            rows_ref[pl.ds(pl.multiple_of(at * cells, cells), cells), :] = unfold(at, xr_buf)
        gate_up = dot(rows_ref[rows, :], wgu_ref[...])
        gate_part = gate_up[:, :ffw]
        up_part = gate_up[:, ffw:]
        sig = jax.nn.sigmoid(gate_part)
        silu = gate_part * sig
        hidden = (silu * up_part).astype(BF16)
        hid_ref[rows, :] = hidden
        out = dot(hidden, wdn_ref[...])
        for n in range(group):
            fold(out[n * cells : (n + 1) * cells], chunk * group + n, ys_buf)

        @pl.when(inner)
        def _():
            exchange(1, 1, chunk, ys_buf, yr_buf, lambda k: behind(k, sec + 1), order_all)

        @pl.when(last)
        def _():
            exchange(1, 4, chunk, ys_buf, yl_buf, behind, order)
            yl_buf[span(chunk), 0:blk] = ys_buf[span(chunk), 0:blk]

        silu_buf[rows, :] = silu
        slope_buf[rows, :] = up_part * (sig * (1.0 + gate_part * (1.0 - sig)))

        @pl.when(chunk == chunks - 1)
        def _():
            stores[0].start()
            stores[1].start()

    piece = width // ne
    me = ey * nz + ez
    my_piece = pl.ds(pl.multiple_of(me * piece, LANES), piece)

    def part_copy(k):
        there = lax.rem(ey + k // nz, ny) * nz + lax.rem(ez + k % nz, nz)
        return pltpu.make_async_remote_copy(
            src_ref=part_s.at[:, pl.ds(pl.multiple_of(there * piece, LANES), piece)],
            dst_ref=part_r.at[k], send_sem=red_send.at[0], recv_sem=red_recv.at[0],
            device_id=ahead(k), device_id_type=MESH,
        )

    def sum_copy(k):
        return pltpu.make_async_remote_copy(
            src_ref=sum_s, dst_ref=sum_r.at[:, my_piece],
            send_sem=red_send.at[1], recv_sem=red_recv.at[1],
            device_id=ahead(k), device_id_type=MESH,
        )

    def gain_copy(k):
        return pltpu.make_async_remote_copy(
            src_ref=gain_s, dst_ref=gain_r.at[k],
            send_sem=red_send.at[2], recv_sem=red_recv.at[2],
            device_id=ahead(k), device_id_type=MESH,
        )

    def slope_of_gates(at, picked, gate_ref, out):
        gates = gate_ref[at][:, :1]
        grad = (g_buf if out is l_buf else gs_buf)[at].astype(F32)
        diff = jnp.sum(grad * (picked[:tok] - picked[tok:]), axis=-1, keepdims=True)
        out[at] = jnp.broadcast_to(gates[:tok] * gates[tok:] * diff, (tok, LANES))

    def route_grads(chunk):
        for n in range(group):
            at = chunk * group + n
            cols = (l_buf[at][:, :1] * sign_ref[at]).astype(BF16)
            dul_buf[at] = dot(cols, router_ref[...])
            acc_r[...] += dot_tn(cols, u_buf[at])

        @pl.when(chunk == chunks - 1)
        def _():
            part_s[...] = acc_r[...].astype(BF16)
            for k in order:
                part_copy(k).start()

    def sum_pieces():
        wait_all(part_r.at[pl.ds(1, ne - 1)], red_recv.at[0])
        total = part_s[:, my_piece].astype(F32)
        for k in range(1, ne):
            total = total + part_r[k].astype(F32)
        sum_s[...] = total
        sum_r[:, my_piece] = total
        for k in order:
            sum_copy(k).start()

    def expert_grads(chunk):
        @pl.when(inner)
        def _():
            all_arrived(2, chunk, dr_buf)

        @pl.when(last)
        def _():
            arrived(2, chunk, dr_buf)

        rows = pl.ds(pl.multiple_of(chunk * group * cells, cells), group * cells)
        for n in range(group):
            at = chunk * group + n
            dyr_ref[pl.ds(pl.multiple_of(at * cells, cells), cells), :] = unfold(at, dr_buf)
        d_hidden = dot_nt(dyr_ref[rows, :], wdn_ref[...])
        q_ref[rows, :ffw] = (d_hidden * slope_buf[rows, :]).astype(BF16)
        q_ref[rows, ffw:] = (d_hidden * silu_buf[rows, :]).astype(BF16)
        out = dot_nt(q_ref[rows, :], wgu_ref[...])
        for n in range(group):
            fold(out[n * cells : (n + 1) * cells], chunk * group + n, us_buf, ur_buf)
        exchange(3, 3, chunk, us_buf, ur_buf, behind, order)

        @pl.when(chunk == chunks - 1)
        def _():
            stores[2].start()
            stores[3].start()

        @pl.when(inner)
        def _():
            down(line_l, chunk).wait_recv()
            route_grads(chunk)

    def gin_copy(chunk, target):
        return pltpu.make_async_remote_copy(
            src_ref=gs_buf.at[span(chunk), :, pl.ds(target * part, part)],
            dst_ref=gin_r.at[span(chunk)],
            send_sem=gin_send.at[target, chunk], recv_sem=gin_recv.at[chunk],
            device_id={"section": target}, device_id_type=MESH,
        )

    def grads(chunk):
        @pl.when(last)
        def _():
            arrived(4, chunk, yl_buf)
            for n in range(group):
                at = chunk * group + n
                slope_of_gates(at, dot(pick(tab, at), unfold(at, yl_buf)), gate_buf, l_buf)
            route_grads(chunk)

        @pl.when(inner)
        def _():
            down(line_g, chunk).wait_recv()

        @pl.when(inner & (chunk == chunks - 1))
        def _():
            sum_pieces()

        arrived(3, chunk, ur_buf)
        for n in range(group):
            at = chunk * group + n
            picked = dot(pick(tab, at), unfold(at, ur_buf))
            grad_u = picked[:tok] + picked[tok:] + dul_buf[at]
            h_wide = h_buf[at].astype(F32)
            inv = inv_rms(h_wide)
            scaled = grad_u * gain_ref[...]
            proj = jnp.mean(scaled * h_wide, axis=-1, keepdims=True)
            grad = g_buf[at].astype(F32) + inv * scaled - h_wide * (inv * inv * inv * proj)
            gs_buf[at] = grad.astype(BF16)
            dul_buf[at] = grad_u

        @pl.when(lower)
        def _():
            for n in range(group):
                at = chunk * group + n
                send_grad(at, gs_buf[at].astype(F32), gatein_buf, tab_in, dn_buf)
            exchange(4, 2, chunk, dn_buf, dr_buf, lambda k: ahead(k, sec - 1), order_all)
            down(line_g, chunk, sec - 1).start()
            for n in range(group):
                at = chunk * group + n
                slope_of_gates(at, pick_buf[at].astype(F32), gatein_buf, ls_buf)
            down(line_l, chunk, sec - 1).start()

        @pl.when(first)
        def _():
            for target in range(1, ns):
                gin_copy(chunk, target).start()
            gin_ref[span(chunk)] = gs_buf[span(chunk), :, 0:part]

        for n in range(group):
            at = chunk * group + n
            h_wide = h_buf[at].astype(F32)
            acc_g[...] += jnp.sum(dul_buf[at] * h_wide * inv_rms(h_wide), axis=0, keepdims=True)

    latest = chunks + LAG - 1
    turn = jnp.minimum(LAG + BETWEEN * (ns - 1 - sec), latest)
    tasks = ((tokens, 0), (experts, LAG), (expert_grads, turn), (grads, turn + LAG))

    def step(i, carry):
        for task, lag in tasks:
            at = i - lag

            @pl.when((at >= 0) & (at < chunks))
            def _():
                task(at)

        return carry

    lax.fori_loop(0, latest + chunks + LAG, step, 0)

    for i in range(ne):
        gain_s[i : i + 1, :] = acc_g[:, i * piece : (i + 1) * piece].astype(BF16)
    for k in order:
        gain_copy(k).start()

    @pl.when(last)
    def _():
        sum_pieces()

    @pl.when(sec != 0)
    def _():
        def take(chunk, carry):
            dst = gin_r.at[span(chunk)]
            pltpu.make_async_copy(dst, dst, gin_recv.at[chunk]).wait()
            return carry

        lax.fori_loop(0, chunks, take, 0)
        gin_ref[...] = gin_r[...]

    sums = sum_r.at[:, pl.ds(0, (ne - 1) * piece)]
    wait_all(sums, red_recv.at[1])
    router_sum_ref[...] = sum_r[...]
    gains = gain_r.at[pl.ds(1, ne - 1)]
    wait_all(gains, red_recv.at[2])
    total = gain_s[...].astype(F32)
    for k in range(1, ne):
        total = total + gain_r[k].astype(F32)
    for i in range(ne):
        gain_sum_ref[:, i * piece : (i + 1) * piece] = total[i : i + 1, :]

    wait_all(part_r.at[pl.ds(1, ne - 1)], red_send.at[0])
    wait_all(sums, red_send.at[1])
    wait_all(gains, red_send.at[2])
    for store in stores:
        store.wait()

    def drain(chunk, carry):
        wait_all(others(xs_buf, chunk), send_sem.at[0, chunk])
        wait_all(others(us_buf, chunk), send_sem.at[3, chunk])

        @pl.when(inner)
        def _():
            wait_all(ys_buf.at[span(chunk)], send_sem.at[1, chunk])
            up(line_h, chunk).wait_send()
            up(line_gate, chunk).wait_send()

        @pl.when(last)
        def _():
            wait_all(others(ys_buf, chunk), send_sem.at[1, chunk])
            wait_all(others(ds_buf, chunk), send_sem.at[2, chunk])

        @pl.when(lower)
        def _():
            wait_all(dn_buf.at[span(chunk)], send_sem.at[4, chunk])
            down(line_g, chunk).wait_send()
            down(line_l, chunk).wait_send()

        @pl.when(first)
        def _():
            for target in range(1, ns):
                gin_copy(chunk, target).wait_send()

        return carry

    lax.fori_loop(0, chunks, drain, 0)

    @pl.when(sec != 0)
    def _():
        gathers[0].wait_send()
        gathers[1].wait_send()

    @pl.when(sec != ns - 1)
    def _():
        gathers[2].wait_send()
        table_copy(0).wait_send()


def weight_grad_kernel(
    steps, rows_ref, q_ref, hid_ref, dyr_ref, gin_ref, router_ref, gain_ref,
    gu_hbm, dn_hbm, gin_out, router_out, gain_out, gu_ref, dn_ref, sem,
):
    def block(lhs, rhs, out, hbm, first, n):
        size = lhs.shape[1] // n

        def copy(i):
            at = pl.ds(pl.multiple_of(i * size, size), size)
            return pltpu.make_async_copy(out.at[at], hbm.at[at], sem.at[first + i])

        def step(i, carry):
            at = pl.ds(pl.multiple_of(i * size, size), size)
            out[at, :] = dot_tn(lhs[:, at], rhs[...])
            copy(i).start()
            return carry

        lax.fori_loop(0, n, step, 0)
        return copy

    gu_copy = block(rows_ref, q_ref, gu_ref, gu_hbm, 0, steps[0])
    dn_copy = block(hid_ref, dyr_ref, dn_ref, dn_hbm, steps[0], steps[1])
    gin_out[...] = gin_ref[...]
    router_out[...] = router_ref[...]
    gain_out[...] = gain_ref[...]
    for i in range(steps[0]):
        gu_copy(i).wait()
    for i in range(steps[1]):
        dn_copy(i).wait()


def local(x_in, cotangent, route_ids, norm_gain, router, w_gate_up, w_down):
    ns, ny, nz = (lax.axis_size(a) for a in ("section", "expert", "dp"))
    micro, tok, part = x_in.shape
    width = part * ns
    ne = ny * nz
    cap = 2 * tok // ne
    cells = ne * cap
    ffw = w_down.shape[2]
    chunks = micro // GROUP
    piece = width // ne
    vmem = pltpu.VMEM
    wire = vmem((micro, cells * width // (2 * LANES), 2 * LANES), BF16)
    rows = vmem((micro, tok, width), BF16)
    dma = pltpu.SemaphoreType.DMA
    stash = (
        ((micro * cells, width), BF16),
        ((micro * cells, 2 * ffw), BF16),
        ((micro * cells, ffw), BF16),
        ((micro * cells, width), BF16),
    )
    scratch = (
        [vmem((width, 2 * ffw), BF16), vmem((ffw, width), BF16)]
        + [vmem(*entry) for entry in stash]
        + [
            vmem((micro, 2 * tok + cells, LANES), BF16),
            vmem((micro, 2 * tok + cells, LANES), BF16),
            vmem((micro, tok, ne), F32),
        ]
        + [rows] * 5
        + [wire] * 10
        + [
            vmem((micro, 2 * tok, width), BF16),
            vmem((micro, 2 * tok, LANES), F32),
            vmem((micro, 2 * tok, LANES), F32),
            vmem((micro, tok, LANES), F32),
            vmem((micro, tok, LANES), F32),
            vmem((micro * cells, ffw), F32),
            vmem((micro * cells, ffw), F32),
            vmem((micro, tok, width), F32),
            vmem((2, cells * width // (2 * LANES), LANES), F32),
            vmem((ne, width), F32),
            vmem((1, width), F32),
            vmem((ne, width), BF16), vmem((ne, ne, piece), BF16),
            vmem((ne, piece), F32), vmem((ne, width), F32),
            vmem((ne, piece), BF16), vmem((ne, ne, piece), BF16),
            vmem((micro, tok, part), BF16),
            dma((5, chunks)), dma((5, chunks)), dma((4, chunks)), dma((4, chunks)), dma((2,)),
            dma((3,)), dma((3,)), dma((ns, chunks)), dma((chunks,)), dma((3,)), dma((3,)), dma((6,)),
        ]
    )
    small = (
        jax.ShapeDtypeStruct((micro, tok, part), BF16),
        jax.ShapeDtypeStruct((ne, width), F32),
        jax.ShapeDtypeStruct((1, width), F32),
    )
    in_vmem = pl.BlockSpec(memory_space=pltpu.VMEM)
    anywhere = pl.BlockSpec(memory_space=pl.ANY)
    *saved, grad_in, sum_router, sum_gain = pl.pallas_call(
        functools.partial(stack_kernel, (ns, ny, nz, cap)),
        out_shape=tuple(jax.ShapeDtypeStruct(*entry) for entry in stash) + small,
        in_specs=[in_vmem] * 5 + [anywhere] * 2,
        out_specs=[anywhere] * 4 + [in_vmem] * 3,
        scratch_shapes=scratch,
        compiler_params=pltpu.CompilerParams(
            collective_id=0, has_side_effects=True, vmem_limit_bytes=60 * 1024 * 1024
        ),
    )(
        x_in, cotangent, jnp.transpose(route_ids[0], (0, 2, 1)), norm_gain, router[0].T,
        w_gate_up[0, 0], w_down[0, 0],
    )
    steps = (width // 256, max(1, ffw // 128))
    grad_gu, grad_dn, grad_in, sum_router, sum_gain = pl.pallas_call(
        functools.partial(weight_grad_kernel, steps),
        out_shape=(
            jax.ShapeDtypeStruct((width, 2 * ffw), F32),
            jax.ShapeDtypeStruct((ffw, width), F32),
        )
        + small,
        in_specs=[in_vmem] * 7,
        out_specs=[anywhere] * 2 + [in_vmem] * 3,
        scratch_shapes=[
            vmem((width, 2 * ffw), F32),
            vmem((ffw, width), F32),
            dma((sum(steps),)),
        ],
        compiler_params=pltpu.CompilerParams(vmem_limit_bytes=40 * 1024 * 1024),
    )(*saved, grad_in, sum_router, sum_gain)
    return grad_in, grad_gu[None, None], grad_dn[None, None], sum_router.T[None], sum_gain


def solution(mesh):
    in_specs = (
        P(None, ("expert", "dp"), "section"),
        P(None, ("expert", "dp"), "section"),
        P("section", None, ("expert", "dp"), None),
        P("section", None),
        P("section", None, None),
        P("section", ("expert", "dp"), None, None),
        P("section", ("expert", "dp"), None, None),
    )
    out_specs = (
        P(None, ("expert", "dp"), "section"),
        P("section", ("expert", "dp"), None, None),
        P("section", ("expert", "dp"), None, None),
        P("section", None, None),
        P("section", None),
    )
    return jax.shard_map(local, mesh=mesh, in_specs=in_specs, out_specs=out_specs, check_vma=False)
```

time: 352 us -> 256 us (0.73)
  Pallas kernels: 338 us -> 248 us
  matrix products: 8.89 us -> 0 us
  local copies, waits for them, and re-layouts: 2.68 us -> 6.87 us
    pallas_call x1, Pallas kernels: 338 us -> 243 us  [local(): pl.pallas_call(functools.partial(stack_kernel, (ns, ny, nz, cap)), out_sh...]
    dot_general x2 -> x0, matrix products: 8.89 us -> none  [dot_tn(): lax.dot_general(lhs, rhs, (((0,), (0,)), ((), ())), preferred_element_typ...]
    unnamed x9 -> x14, local copies, waits for them, and re-layouts: 0.65 us -> 6.87 us
    pallas_call x0 -> x1, Pallas kernels: none -> 5.8 us  [local(): pl.pallas_call(functools.partial(weight_grad_kernel, steps), out_shape=(j...]
where the time goes in v2:
time: 256 us
  Pallas kernels  248 us (97%)
  local copies, waits for them, and re-layouts  6.87 us (3%)
    pallas_call x1, Pallas kernels, local(): pl.pallas_call(functools.partial(stack_kernel, (ns, ny, nz, cap)), out_sh...  243 us
    unnamed x14, local copies, waits for them, and re-layouts  6.87 us
    pallas_call x1, Pallas kernels, local(): pl.pallas_call(functools.partial(weight_grad_kernel, steps), out_shape=(j...  5.8 us

profile of v2, /device:TPU:0, one launch (start us, length us, event | category | flops | bytes accessed | tf_op | source)
XLA Modules:
  0.0 255.9 jit_solution(12774245486699698159)
XLA Ops:
  0.6 242.6 %shard_map.110 = (bf16[256,2048]{1,0:T(8,128)(2,1)}, bf16[256,1024]{1,0:T(8,128)(2,1)}, bf16[256,512]{1,0:T(8,128)(2,1)}, bf16[256,2048]{1,0:T(8,128)(2,1)}, bf1...) custom-call(bf16[8,16,256]{2,1,0:T(8,128)(2,1)} %x_ref.1, bf16[8,16,256]{2,1,0:T(8,128)(2,1)} %cot_ref.1, ...), custom_call_target="tpu_custom_call" | custom-call | tf_op jit(solution)/shard_map/pallas_call | solution.py:677
  243.2 0.0 copy-start
  243.2 1.2 copy-done
  244.4 0.0 copy-start.1
  244.4 1.2 copy-done.1
  245.7 0.0 copy-start.2
  245.7 1.0 copy-done.2
  246.7 0.0 copy-start.3
  246.7 0.9 copy-done.3
  247.6 0.0 copy-start.4
  247.7 0.9 copy-done.4
  248.6 0.0 copy-start.5
  248.6 0.8 copy-done.5
  249.4 0.0 copy-start.6
  249.4 0.7 copy-done.6
  250.1 5.8 %shard_map.111 = (f32[2048,1024]{1,0:T(8,128)}, f32[512,2048]{1,0:T(8,128)}, bf16[8,16,256]{2,1,0:T(8,128)(2,1)}, f32[16,2048]{1,0:T(8,128)}, f32[1,2048]{1,0:T(1,128)}) custom-call(bf16[256,2048]{1,0:T(8,128)(2,1)S(1)} %copy-done, bf16[256,1024]{1,0:T(8,128)(2,1)S(1)} %copy-done.2, bf16[256,512]{1,0:T(8,128)(2,1)S(1)} %copy-done.3, ...), custom_call_target="tpu_custom_call" | custom-call | tf_op jit(solution)/shard_map/pallas_call | solution.py:691
Async XLA Ops:
  243.2 1.2 copy-start
  244.4 1.2 copy-start.1
  245.7 1.0 copy-start.2
  246.7 0.9 copy-start.3
  247.6 0.9 copy-start.4
  248.6 0.8 copy-start.5
  249.4 0.7 copy-start.6

commit v3 on v2

--- a/solution.py
+++ b/solution.py
@@ -33,7 +33,7 @@
     sizes,
     x_ref, cot_ref, route_ref, gain_ref, router_ref, wgu_hbm, wdn_hbm,
     rows_hbm, q_hbm, hid_hbm, dyr_hbm, gin_ref, router_sum_ref, gain_sum_ref,
-    wgu_ref, wdn_ref, rows_ref, q_ref, hid_ref, dyr_ref, tab, tab_in, sign_ref,
+    wgu_ref, wdn_ref, wgu_t, wdn_t, rows_ref, q_ref, hid_ref, dyr_ref, tab, tab_in, sign_ref,
     h_buf, hin_buf, g_buf, u_buf, gs_buf,
     xs_buf, xr_buf, ys_buf, yr_buf, yl_buf, ds_buf, dn_buf, dr_buf, us_buf, ur_buf,
     pick_buf, gate_buf, gatein_buf, l_buf, ls_buf, slope_buf, silu_buf, dul_buf, wide,
@@ -246,6 +246,25 @@
         pair = (gs_buf, g_buf) if way == line_g else (ls_buf, l_buf)
         return line_copy(way, chunk, *pair, target)
 
+    def turn_weights():
+        for src, dst in ((wgu_ref, wgu_t), (wdn_ref, wdn_t)):
+            size = min(2 * LANES, src.shape[1])
+            one = eye(size)
+
+            def turn(j, carry, src=src, dst=dst, size=size, one=one):
+                at = pl.ds(pl.multiple_of(j * size, size), size)
+                dst[at, :] = dot_nt(one, src[:, at]).astype(BF16)
+                return carry
+
+            lax.fori_loop(0, src.shape[1] // size, turn, 0)
+
+    for load in loads:
+        load.wait()
+
+    @pl.when(sec >= ns // 2)
+    def _():
+        turn_weights()
+
     def tokens(chunk):
         @pl.when(first & (chunk == 0))
         def _():
@@ -308,11 +327,6 @@
         fold(dot(put(table, at), scaled), at, send, recv)
 
     def experts(chunk):
-        @pl.when(chunk == 0)
-        def _():
-            for load in loads:
-                load.wait()
-
         arrived(0, chunk, xr_buf)
         rows = pl.ds(pl.multiple_of(chunk * group * cells, cells), group * cells)
         for n in range(group):
@@ -346,6 +360,10 @@
             stores[0].start()
             stores[1].start()
 
+        @pl.when((chunk == chunks - 1) & (sec < ns // 2))
+        def _():
+            turn_weights()
+
     piece = width // ne
     me = ey * nz + ez
     my_piece = pl.ds(pl.multiple_of(me * piece, LANES), piece)
@@ -414,10 +432,10 @@
         for n in range(group):
             at = chunk * group + n
             dyr_ref[pl.ds(pl.multiple_of(at * cells, cells), cells), :] = unfold(at, dr_buf)
-        d_hidden = dot_nt(dyr_ref[rows, :], wdn_ref[...])
+        d_hidden = dot(dyr_ref[rows, :], wdn_t[...])
         q_ref[rows, :ffw] = (d_hidden * slope_buf[rows, :]).astype(BF16)
         q_ref[rows, ffw:] = (d_hidden * silu_buf[rows, :]).astype(BF16)
-        out = dot_nt(q_ref[rows, :], wgu_ref[...])
+        out = dot(q_ref[rows, :], wgu_t[...])
         for n in range(group):
             fold(out[n * cells : (n + 1) * cells], chunk * group + n, us_buf, ur_buf)
         exchange(3, 3, chunk, us_buf, ur_buf, behind, order)
@@ -587,9 +605,23 @@
 
 
 def weight_grad_kernel(
-    steps, rows_ref, q_ref, hid_ref, dyr_ref, gin_ref, router_ref, gain_ref,
-    gu_hbm, dn_hbm, gin_out, router_out, gain_out, gu_ref, dn_ref, sem,
+    steps, rows_hbm, q_hbm, hid_hbm, dyr_hbm, gin_hbm, router_hbm, gain_hbm,
+    gu_hbm, dn_hbm, gin_out, router_out, gain_out,
+    rows_ref, q_ref, hid_ref, dyr_ref, gin_ref, router_ref, gain_ref, gu_ref, dn_ref, sem, load_sem, pass_sem,
 ):
+    sources = (rows_hbm, q_hbm, hid_hbm, dyr_hbm, gin_hbm, router_hbm, gain_hbm)
+    landings = (rows_ref, q_ref, hid_ref, dyr_ref, gin_ref, router_ref, gain_ref)
+    loads = [
+        pltpu.make_async_copy(src, dst, load_sem.at[n])
+        for n, (src, dst) in enumerate(zip(sources, landings))
+    ]
+    passes = [
+        pltpu.make_async_copy(src, dst, pass_sem.at[n])
+        for n, (src, dst) in enumerate(zip(landings[4:], (gin_out, router_out, gain_out)))
+    ]
+    for load in loads:
+        load.start()
+
     def block(lhs, rhs, out, hbm, first, n):
         size = lhs.shape[1] // n
 
@@ -606,15 +638,20 @@
         lax.fori_loop(0, n, step, 0)
         return copy
 
+    loads[0].wait()
+    loads[1].wait()
     gu_copy = block(rows_ref, q_ref, gu_ref, gu_hbm, 0, steps[0])
+    for load in loads[2:]:
+        load.wait()
+    for onward in passes:
+        onward.start()
     dn_copy = block(hid_ref, dyr_ref, dn_ref, dn_hbm, steps[0], steps[1])
-    gin_out[...] = gin_ref[...]
-    router_out[...] = router_ref[...]
-    gain_out[...] = gain_ref[...]
     for i in range(steps[0]):
         gu_copy(i).wait()
     for i in range(steps[1]):
         dn_copy(i).wait()
+    for onward in passes:
+        onward.wait()
 
 
 def local(x_in, cotangent, route_ids, norm_gain, router, w_gate_up, w_down):
@@ -639,6 +676,7 @@
     )
     scratch = (
         [vmem((width, 2 * ffw), BF16), vmem((ffw, width), BF16)]
+        + [vmem((2 * ffw, width), BF16), vmem((width, ffw), BF16)]
         + [vmem(*entry) for entry in stash]
         + [
             vmem((micro, 2 * tok + cells, LANES), BF16),
@@ -695,14 +733,18 @@
             jax.ShapeDtypeStruct((ffw, width), F32),
         )
         + small,
-        in_specs=[in_vmem] * 7,
-        out_specs=[anywhere] * 2 + [in_vmem] * 3,
-        scratch_shapes=[
+        in_specs=[anywhere] * 7,
+        out_specs=[anywhere] * 5,
+        scratch_shapes=[vmem(*entry) for entry in stash]
+        + [vmem(entry.shape, entry.dtype) for entry in small]
+        + [
             vmem((width, 2 * ffw), F32),
             vmem((ffw, width), F32),
             dma((sum(steps),)),
+            dma((7,)),
+            dma((3,)),
         ],
-        compiler_params=pltpu.CompilerParams(vmem_limit_bytes=40 * 1024 * 1024),
+        compiler_params=pltpu.CompilerParams(vmem_limit_bytes=60 * 1024 * 1024),
     )(*saved, grad_in, sum_router, sum_gain)
     return grad_in, grad_gu[None, None], grad_dn[None, None], sum_router.T[None], sum_gain
 

time: 256 us -> 239 us (0.934)
  Pallas kernels: 248 us -> 239 us
  local copies, waits for them, and re-layouts: 6.87 us -> 0 us
    pallas_call x1, Pallas kernels: 243 us -> 232 us  [local(): pl.pallas_call(functools.partial(stack_kernel, (ns, ny, nz, cap)), out_sh...]
    unnamed x14 -> x0, local copies, waits for them, and re-layouts: 6.87 us -> none
where the time goes in v3:
time: 239 us
  Pallas kernels  239 us (100%)
    pallas_call x1, Pallas kernels, local(): pl.pallas_call(functools.partial(stack_kernel, (ns, ny, nz, cap)), out_sh...  232 us
    pallas_call x1, Pallas kernels, local(): pl.pallas_call(functools.partial(weight_grad_kernel, steps), out_shape=(j...  6.59 us

profile of v3, /device:TPU:0, one launch (start us, length us, event | category | flops | bytes accessed | tf_op | source)
XLA Modules:
  0.0 239.3 jit_solution(2562482759522522629)
XLA Ops:
  0.6 232.0 %shard_map.110 = (bf16[256,2048]{1,0:T(8,128)(2,1)}, bf16[256,1024]{1,0:T(8,128)(2,1)}, bf16[256,512]{1,0:T(8,128)(2,1)}, bf16[256,2048]{1,0:T(8,128)(2,1)}, bf1...) custom-call(bf16[8,16,256]{2,1,0:T(8,128)(2,1)} %x_ref.1, bf16[8,16,256]{2,1,0:T(8,128)(2,1)} %cot_ref.1, ...), custom_call_target="tpu_custom_call" | custom-call | tf_op jit(solution)/shard_map/pallas_call | solution.py:715
  232.7 6.6 %shard_map.111 = (f32[2048,1024]{1,0:T(8,128)}, f32[512,2048]{1,0:T(8,128)}, bf16[8,16,256]{2,1,0:T(8,128)(2,1)}, f32[16,2048]{1,0:T(8,128)}, f32[1,2048]{1,0:T(1,128)}) custom-call(bf16[256,2048]{1,0:T(8,128)(2,1)} %get-tuple-element.17.rows_hbm, bf16[256,1024]{1,0:T(8,128)(2,1)} %get-tuple-element.18.q_hbm, bf16[256,512]{1,0:T(8,128)(2,1)} %get-tuple-element.19.hid_hbm, ...), custom_call_target="tpu_custom_call" | custom-call | tf_op jit(solution)/shard_map/pallas_call | solution.py:729
